TPU v7x, 32 devices: a whole 2x2x4 slice. The times are simulated.
32 devices in a mesh: dp: 1, ep: 32 (over x, y, z, core).
Axes of the slice: x: 2, y: 2, z: 4, core: 2. Of those that a mesh axis runs over, the one named last changes fastest.
Arguments:
- x: bfloat16 [1, 32, 256, 1792], P('dp', 'ep')
- expert: int32 [1, 32, 256, 8], P('dp', 'ep')
- slot: int32 [1, 32, 256, 8], P('dp', 'ep')
- gate: float32 [1, 32, 256, 8], P('dp', 'ep')
- w_gate: bfloat16 [64, 1792, 2560], P('ep')
- w_up: bfloat16 [64, 1792, 2560], P('ep')
- w_down: bfloat16 [64, 2560, 1792], P('ep')
- s_gate: bfloat16 [1792, 20480], replicated
- s_up: bfloat16 [1792, 20480], replicated
- s_down: bfloat16 [20480, 1792], replicated
Outputs:
- y: bfloat16 [1, 32, 256, 1792], P('dp', 'ep')
All inputs are finite; a program needn't handle non-finite values.
Results may differ from a plain program's by a relative error of at most 0.009.
Values are sent between devices in bfloat16 or wider.
A program may use at most 2 GiB of HBM per device.

v0:
```python
import jax
import jax.numpy as jnp
from jax import lax
from jax.sharding import NamedSharding, PartitionSpec as P


def einsum(form, a, b):
    return jnp.einsum(form, a.astype(jnp.float32), b.astype(jnp.float32))


def for_all(x, s_gate, s_up, s_down):
    h = jax.nn.silu(einsum("...d,df->...f", x, s_gate)) * einsum("...d,df->...f", x, s_up)
    return einsum("...f,fd->...d", h.astype(jnp.bfloat16), s_down)


def solution(mesh):
    def placed(v, *spec):
        return lax.with_sharding_constraint(v, NamedSharding(mesh, P(*spec)))

    def step(x, expert, slot, gate, w_gate, w_up, w_down, s_gate, s_up, s_down):
        experts, (tokens, top) = w_gate.shape[0], expert.shape[2:]
        slots = 5 * tokens * top // (4 * experts)
        to_expert = jax.nn.one_hot(expert, experts, dtype=jnp.bfloat16)
        to_slot = jax.nn.one_hot(slot, slots, dtype=jnp.bfloat16)
        weighted = to_expert * gate[..., None].astype(jnp.bfloat16)
        dispatch = einsum("abtke,abtkc->abtec", to_expert, to_slot).astype(jnp.bfloat16)
        combine = einsum("abtke,abtkc->abtec", weighted, to_slot).astype(jnp.bfloat16)
        z = einsum("abtec,abtd->aebcd", dispatch, x).astype(jnp.bfloat16)
        z = placed(z, "dp", None, "ep", None, None)
        z = placed(z, "dp", "ep", None, None, None)
        h = jax.nn.silu(einsum("aebcd,edf->aebcf", z, w_gate))
        h = (h * einsum("aebcd,edf->aebcf", z, w_up)).astype(jnp.bfloat16)
        out = einsum("aebcf,efd->aebcd", h, w_down).astype(jnp.bfloat16)
        out = placed(out, "dp", "ep", None, None, None)
        out = placed(out, "dp", None, "ep", None, None)
        y = einsum("abtec,aebcd->abtd", combine, out)
        return (y + for_all(x, s_gate, s_up, s_down)).astype(jnp.bfloat16)

    return step
```

profile of v0, /device:TPU:0, one launch (start us, length us, event | category | flops | bytes accessed | tf_op | source)
XLA Modules:
  0.0 548.1 jit_solution(17267040932048846699)
XLA Ops:
  0.0 0.0 copy-start
  0.0 0.9 copy.10
  0.9 0.0 copy-start.1
  0.9 0.8 copy.12
  1.8 0.0 copy-done.1
  1.8 0.0 copy-start.3
  1.8 0.6 copy-done.3
  2.4 3.6 convolution_convert_fusion.1
  6.1 5.6 %copy.13 = bf16[256,64,40]{0,2,1:T(8,128)(2,1)S(1)} copy(bf16[256,64,40]{1,2,0:T(8,128)(2,1)} %convolution_convert_fusion.1) | data formatting | bytes 2621440 | tf_op jit(solution)/convert_element_type | solution.py:26
  11.7 0.0 copy-done
  11.7 2.6 convolution_convert_fusion
  14.3 210.9 %all-to-all.4 = bf16[1,32,2,1,40,1792]{5,4,2,3,0,1:T(8,128)(2,1)} all-to-all(bf16[1,32,2,1,40,1792]{5,4,2,3,0,1:T(8,128)(2,1)S(1)} %bitcast.150), channel_id=1, replica_groups=mesh['dp'=1,'ep'=32] {'ep'}, dimensions={1} | all-to-all | bytes 18350080 | tf_op jit(solution)/sharding_constraint;jit(solution)/sharding_constraint | solution.py:18
  225.2 32.3 %fusion.9 = f32[2,32,40,2560]{3,2,1,0:T(8,128)} fusion(bf16[2,1792,2560]{2,1,0:T(8,128)(2,1)} %param.5, bf16[1,32,2,1,40,1792]{5,4,2,3,0,1:T(8,128)(2,1)} %all-to-all.4), kind=kOutput, calls=%fused_computation.14 | convolution fusion | flops 23488102400 | bytes 53739520 | tf_op jit(solution)/aebcd,edf->aebcf/dot_general | solution.py:8
  257.5 35.7 %fusion.1 = bf16[1,2,32,40,2560]{4,3,2,1,0:T(8,128)(2,1)} fusion(f32[2,32,40,2560]{3,2,1,0:T(8,128)} %fusion.9, bf16[2,1792,2560]{2,1,0:T(8,128)(2,1)} %param.4, bf16[1,32,2,1,40,1792]{5,4,2,3,0,1:T(8,128)(2,1)} %all-to-all.4), kind=kOutput, calls=%fused_computation.4 | convolution fusion | flops 23527424000 | bytes 66846720 | tf_op jit(solution)/aebcd,edf->aebcf/dot_general | solution.py:8
  293.2 32.5 %convert_bitcast_fusion = bf16[1,2,32,1,40,1792]{5,4,2,1,3,0:T(8,128)(2,1)} fusion(bf16[2,2560,1792]{2,1,0:T(8,128)(2,1)} %param.6, bf16[1,2,32,40,2560]{4,3,2,1,0:T(8,128)(2,1)} %fusion.1), kind=kOutput, calls=%fused_computation.21 | convolution fusion | flops 23492689920 | bytes 40632320 | tf_op jit(solution)/aebcf,efd->aebcd/dot_general | solution.py:8
  325.7 0.0 copy-start.5
  325.7 0.0 copy-start.2
  325.7 0.0 copy-start.4
  325.7 7.8 %copy.16 = bf16[1,2,32,1,40,1792]{5,4,1,3,0,2:T(8,128)(2,1)} copy(bf16[1,2,32,1,40,1792]{5,4,2,1,3,0:T(8,128)(2,1)} %convert_bitcast_fusion) | data formatting | bytes 18350080 | tf_op jit(solution)/sharding_constraint;jit(solution)/sharding_constraint | solution.py:18
  333.5 4.9 all-to-all-start.1
  338.4 0.0 copy-done.5
  338.4 0.1 copy.11
  338.6 0.0 copy-done.2
  338.6 0.0 copy-done.4
  338.6 4.3 convolution_convert_fusion.2
  342.9 5.6 %copy.23 = bf16[256,64,40]{0,2,1:T(8,128)(2,1)S(1)} copy(bf16[256,64,40]{1,2,0:T(8,128)(2,1)} %convolution_convert_fusion.2) | data formatting | bytes 2621440 | tf_op jit(solution)/convert_element_type | solution.py:27
  348.5 38.0 %convolution_bitcast_fusion.1 = f32[1,256,20480]{2,1,0:T(8,128)} fusion(bf16[1792,20480]{1,0:T(8,128)(2,1)} %param.7, bf16[1,1,256,1792]{3,2,1,0:T(8,128)(2,1)S(1)} %copy-done), kind=kOutput, calls=%fused_computation.1 | convolution fusion | flops 18790481920 | bytes 95289344 | tf_op jit(solution)/...d,df->...f/dot_general | solution.py:8
  386.5 37.0 %fusion.6.clone.4 = bf16[256,20480]{1,0:T(8,128)(2,1)} fusion(bf16[1792,20480]{1,0:T(8,128)(2,1)} %param.8, f32[1,256,20480]{2,1,0:T(8,128)} %convolution_bitcast_fusion.1, bf16[1,1,256,1792]{3,2,1,0:T(8,128)(2,1)S(1)} %copy-done), kind=kOutput, calls=%fused_computation.11.clone.clone.clone.1 | convolution fusion | flops 18821939200 | bytes 105775104 | tf_op jit(solution)/...d,df->...f/dot_general | solution.py:8
  423.5 31.5 %fusion.24 = f32[256,1792]{1,0:T(8,128)} fusion(bf16[20480,1792]{1,0:T(8,128)(2,1)} %param.9, bf16[256,20480]{1,0:T(8,128)(2,1)} %fusion.6.clone.4), kind=kOutput, calls=%fused_computation.25 | convolution fusion | flops 18790481920 | bytes 85721088 | tf_op jit(solution)/...f,fd->...d/dot_general | solution.py:8
  454.9 85.3 %all-to-all-done.1 = bf16[1,2,32,1,40,1792]{5,4,1,3,0,2:T(8,128)(2,1)} async-done(((bf16[1,2,32,1,40,1792]{5,4,1,3,0,2:T(8,128)(2,1)}), bf16[1,2,32,1,40,1792]{5,4,1,3,0,2:T(8,128)(2,1)}, u32[]{:S(2)}, u32[]{:S(2)}) %all-to-all-start.1) | async-done | bytes 9175072 | tf_op jit(solution)/sharding_constraint;jit(solution)/sharding_constraint | solution.py:18
  540.3 7.6 %fusion.27 = bf16[1,1,256,1792]{3,2,1,0:T(8,128)(2,1)} fusion(f32[256,1792]{1,0:T(8,128)} %fusion.24, bf16[256,64,40]{0,2,1:T(8,128)(2,1)S(1)} %copy.23, bf16[64,40,1792]{2,1,0:T(8,128)(2,1)} %bitcast.38), kind=kOutput, calls=%fused_computation.29 | convolution fusion | flops 2349727744 | bytes 13238272 | tf_op jit(solution)/abtec,aebcd->abtd/dot_general | solution.py:8
  (1 shorter events, 0.0 us)
Async XLA Ops:
  0.0 11.7 %copy-start = (bf16[1,1,256,1792]{3,2,1,0:T(8,128)(2,1)S(1)}, bf16[1,1,256,1792]{3,2,1,0:T(8,128)(2,1)}, u32[]{:S(2)}) copy-start(bf16[1,1,256,1792]{3,2,1,0:T(8,128)(2,1)} %param.3) | copy-start | bytes 2752516
  0.9 0.9 copy-start.1
  1.8 0.7 copy-start.3
  325.7 12.7 %copy-start.5 = (f32[1,1,256,8]{2,3,1,0:T(8,128)S(1)}, f32[1,1,256,8]{2,3,1,0:T(8,128)}, u32[]{:S(2)}) copy-start(f32[1,1,256,8]{2,3,1,0:T(8,128)} %param.1) | copy-start | bytes 24580
  325.7 12.9 %copy-start.2 = (s32[256,8]{1,0:T(8,128)S(1)}, s32[256,8]{1,0:T(8,128)}, u32[]{:S(2)}) copy-start(s32[256,8]{1,0:T(8,128)} %copy-done.1) | copy-start | bytes 24580
  325.7 12.9 %copy-start.4 = (s32[256,8]{1,0:T(8,128)S(1)}, s32[256,8]{1,0:T(8,128)}, u32[]{:S(2)}) copy-start(s32[256,8]{1,0:T(8,128)} %copy-done.3) | copy-start | bytes 24580
  333.5 206.7 %all-to-all-start.1 = ((bf16[1,2,32,1,40,1792]{5,4,1,3,0,2:T(8,128)(2,1)}), bf16[1,2,32,1,40,1792]{5,4,1,3,0,2:T(8,128)(2,1)}, u32[]{:S(2)}, u32[]{:S(2)}) async-start(bf16[1,2,32,1,40,1792]{5,4,1,3,0,2:T(8,128)(2,1)} %copy.16), calls=%async_computation.1 | async-start | bytes 18350080 | tf_op jit(solution)/sharding_constraint;jit(solution)/sharding_constraint | solution.py:18
where the time goes:
time: 552 us; the launch traced here: 548 us
  matrix products  225 us (41%)
  blocking collectives  211 us (38%)
  waiting for transfers between devices  85.3 us (15%)
  local copies, waits for them, and re-layouts  21.6 us (4%)
    dot_general x10, matrix products, einsum(): return jnp.einsum(form, a.astype(jnp.float32), b.astype(jnp.float32))  225 us
    another operation x1, blocking collectives, placed(): return lax.with_sharding_constraint(v, NamedSharding(mesh, P(*spec)))  211 us
    another operation x1, waiting for transfers between devices, placed(): return lax.with_sharding_constraint(v, NamedSharding(mesh, P(*spec)))  85.3 us
  transfers between devices with their start and end apart: 1, of which 1 were waited for; matrix products, arithmetic and copies ran while one was open for 21% of the time, Pallas kernels for 0%

commit v1 on v0

v1 whole, which is shorter than its diff:
```python
import functools

import jax
import jax.numpy as jnp
from jax import lax
from jax.experimental import pallas as pl
from jax.experimental.pallas import tpu as pltpu
from jax.sharding import PartitionSpec as P


ZS = 4
PLANE = 8
PAIRS = ((1, 2), (3, 0))
BACK = ((1, 2), (3,), (0,))
SHARED_TILE = 1024
EXPERT_TILE = 512
VMEM = 60 * 2**20


def dot(form, a, b):
    return jnp.einsum(form, a, b, preferred_element_type=jnp.float32)


def mm(a, b):
    return jnp.dot(a, b, preferred_element_type=jnp.float32)


def shared_kernel(z_ref, x_ref, g_ref, u_ref, d_ref, o_ref):
    h = (jax.nn.silu(mm(x_ref[...], g_ref[...])) * mm(x_ref[...], u_ref[...])).astype(jnp.bfloat16)

    @pl.when(pl.program_id(0) == 0)
    def _():
        o_ref[...] = mm(h, d_ref[...])

    @pl.when(pl.program_id(0) > 0)
    def _():
        o_ref[...] += mm(h, d_ref[...])


def shared_part(z, x, s_gate, s_up, s_down):
    rows, d = x.shape
    tile = SHARED_TILE
    steps = s_gate.shape[1] // (ZS * tile)
    return pl.pallas_call(
        shared_kernel,
        grid_spec=pltpu.PrefetchScalarGridSpec(
            num_scalar_prefetch=1,
            grid=(steps,),
            in_specs=[
                pl.BlockSpec((rows, d), lambda i, z: (0, 0)),
                pl.BlockSpec((d, tile), lambda i, z: (0, i + z[0] * steps)),
                pl.BlockSpec((d, tile), lambda i, z: (0, i + z[0] * steps)),
                pl.BlockSpec((tile, d), lambda i, z: (i + z[0] * steps, 0)),
            ],
            out_specs=pl.BlockSpec((rows, d), lambda i, z: (0, 0)),
        ),
        out_shape=jax.ShapeDtypeStruct((rows, d), jnp.float32),
        compiler_params=pltpu.CompilerParams(vmem_limit_bytes=VMEM, dimension_semantics=("arbitrary",)),
        cost_estimate=pl.CostEstimate(
            flops=6 * rows * d * tile * steps, bytes_accessed=6 * d * tile * steps, transcendentals=rows * tile * steps
        ),
        name="shared",
    )(z.reshape(1), x, s_gate, s_up, s_down)


def expert_kernel(count, *refs):
    v_refs, (g_ref, u_ref, d_ref), o_refs = refs[:count], refs[count : count + 3], refs[count + 3 : -2]
    held, acc = refs[-2:]
    d = held.shape[-1]
    part = held.shape[0] // count
    f = pl.program_id(1)

    @pl.when(f == 0)
    def _():
        for j, v_ref in enumerate(v_refs):
            held[pl.ds(j * part, part)] = v_ref[...].reshape(part, d)

    v = held[...]
    h = (jax.nn.silu(mm(v, g_ref[0])) * mm(v, u_ref[0])).astype(jnp.bfloat16)
    y = mm(h, d_ref[0])

    @pl.when(f == 0)
    def _():
        acc[...] = y

    @pl.when(f > 0)
    def _():
        acc[...] += y

    @pl.when(f == pl.num_programs(1) - 1)
    def _():
        shape = v_refs[0].shape
        for j in range(count):
            out = acc[pl.ds(j * part, part)].astype(jnp.bfloat16).reshape(shape)
            if len(o_refs) == 1:
                o_refs[0][:, :, pl.ds(j * shape[2], shape[2])] = out
            else:
                o_refs[j][...] = out


def experts_of(vs, w_gate, w_up, w_down, joined):
    senders, mine, slots, d = vs[0].shape
    rows = len(vs) * senders * slots
    ff = w_gate.shape[-1]
    tile = EXPERT_TILE
    block = pl.BlockSpec((senders, 1, slots, d), lambda e, f: (0, e, 0, 0))
    outs = 1 if joined else len(vs)
    wide = slots * len(vs) // outs
    return pl.pallas_call(
        functools.partial(expert_kernel, len(vs)),
        grid=(mine, ff // tile),
        in_specs=[block] * len(vs)
        + [
            pl.BlockSpec((1, d, tile), lambda e, f: (e, 0, f)),
            pl.BlockSpec((1, d, tile), lambda e, f: (e, 0, f)),
            pl.BlockSpec((1, tile, d), lambda e, f: (e, f, 0)),
        ],
        out_specs=[pl.BlockSpec((senders, 1, wide, d), lambda e, f: (0, e, 0, 0))] * outs,
        out_shape=[jax.ShapeDtypeStruct((senders, mine, wide, d), jnp.bfloat16)] * outs,
        scratch_shapes=[pltpu.VMEM((rows, d), jnp.bfloat16), pltpu.VMEM((rows, d), jnp.float32)],
        compiler_params=pltpu.CompilerParams(vmem_limit_bytes=VMEM, dimension_semantics=("arbitrary", "arbitrary")),
        cost_estimate=pl.CostEstimate(
            flops=6 * mine * rows * d * ff, bytes_accessed=6 * mine * d * ff, transcendentals=mine * rows * ff
        ),
        name="experts",
    )(*vs, w_gate, w_up, w_down)


def solution(mesh):
    n = mesh.shape["ep"]
    planes = [[16 * x + 8 * y + 2 * z + c for x in (0, 1) for y in (0, 1) for c in (0, 1)] for z in range(ZS)]

    def shift(v, k):
        return lax.ppermute(v, "ep", [(i, i ^ (2 * k)) for i in range(n)])

    def exchange(v):
        return lax.all_to_all(v, "ep", 0, 0, axis_index_groups=planes, tiled=True)

    def body(x, expert, slot, gate, w_gate, w_up, w_down, s_gate, s_up, s_down):
        x, expert, slot, gate = x[0, 0], expert[0, 0], slot[0, 0], gate[0, 0]
        tokens, top = expert.shape
        mine = w_gate.shape[0]
        slots = 5 * tokens * top // (4 * mine * n)
        rows = PLANE * mine * slots
        z = (lax.axis_index("ep") >> 1) & (ZS - 1)

        route = jnp.concatenate([expert, jnp.minimum(slot, slots)], 1).astype(jnp.bfloat16)
        route = jnp.concatenate([route, gate.astype(jnp.bfloat16)], 1).T
        routes = [route] + [shift(route, k) for k in range(1, ZS)]
        xs = [x]
        for k in range(1, ZS):
            xs.append(shift(x, k))

        def place(r):
            e, s = r[:top].astype(jnp.int32), r[top : 2 * top].astype(jnp.int32)
            d, i = e >> 1, e & 1
            p = ((d >> 4) << 2) | (((d >> 3) & 1) << 1) | (d & 1)
            row = (p * mine + i) * slots + s
            return jnp.where((((d >> 1) & (ZS - 1)) == z) & (s < slots), row, -1)

        sent, combine = [], []
        here = lax.broadcasted_iota(jnp.int32, (rows, tokens), 0)
        for k in range(ZS):
            row = place(routes[k])
            g = routes[k][2 * top :].astype(jnp.float32)
            pick = here == row[0]
            weight = jnp.where(here == row[0], g[0], 0.0)
            for j in range(1, top):
                hit = here == row[j]
                pick = pick | hit
                weight = jnp.where(hit, g[j], weight)
            combine.append(weight.astype(jnp.bfloat16))
            sent.append(dot("rt,td->rd", pick.astype(jnp.bfloat16), xs[k]).astype(jnp.bfloat16).reshape(PLANE, mine, slots, -1))

        got = [exchange(v) for v in sent]
        outs = []
        for i, pair in enumerate(PAIRS):
            outs += experts_of([got[k] for k in pair], w_gate, w_up, w_down, joined=i == 0)

        shared = []
        for k in range(ZS):
            shared.append(shared_part(z, xs[k], s_gate, s_up, s_down))
        total = shared[0]
        for i, group in enumerate(BACK):
            v = exchange(outs[i])
            for j, k in enumerate(group):
                back = v[:, :, j * slots : (j + 1) * slots].reshape(rows, -1)
                part = dot("rt,rd->td", combine[k], back)
                if k:
                    part = shift((part + shared[k]).astype(jnp.bfloat16), k)
                    part = part.astype(jnp.float32)
                total = total + part
        return total.astype(jnp.bfloat16)[None, None]

    tok, exp, rep = P("dp", "ep"), P("ep"), P()

    return jax.shard_map(
        body,
        mesh=mesh,
        in_specs=(tok, tok, tok, tok, exp, exp, exp, rep, rep, rep),
        out_specs=tok,
        check_vma=False,
    )
```

time: 552 us -> 412 us (0.75)
  blocking collectives: 211 us -> 0 us
  matrix products: 225 us -> 21.8 us
  Pallas kernels: 0 us -> 198 us
  starting transfers between devices: 4.91 us -> 54.4 us
  waiting for transfers between devices: 85.3 us -> 120 us
  local copies, waits for them, and re-layouts: 21.6 us -> 11 us
    another operation x1 -> x0, blocking collectives: 211 us -> none  [placed(): return lax.with_sharding_constraint(v, NamedSharding(mesh, P(*spec)))]
    dot_general x10 -> x8, matrix products: 225 us -> 21.8 us  [dot(): return jnp.einsum(form, a, b, preferred_element_type=jnp.float32)]
    pallas_call x0 -> x6, Pallas kernels: none -> 198 us  [the longest x4 100 us: shared_part(): pl.pallas_call(shared_kernel, grid_spec=pltpu.PrefetchScalarGridSpec(num_...]
    ppermute x0 -> x9, waiting for transfers between devices: none -> 119 us  [shift(): return lax.ppermute(v, 'ep', [(i, i ^ 2 * k) for i in range(n)])]
    another operation x1 -> x0, waiting for transfers between devices: 85.3 us -> none  [placed(): return lax.with_sharding_constraint(v, NamedSharding(mesh, P(*spec)))]
    all_to_all x0 -> x7, starting transfers between devices: none -> 31 us  [exchange(): return lax.all_to_all(v, 'ep', 0, 0, axis_index_groups=planes, tiled=True)]
    ppermute x0 -> x9, starting transfers between devices: none -> 23.4 us  [shift(): return lax.ppermute(v, 'ep', [(i, i ^ 2 * k) for i in range(n)])]
    convert_element_type x3 -> x0, local copies, waits for them, and re-layouts: 11.4 us -> none  [the longest x1 5.62 us: step(): einsum('abtke,abtkc->abtec', weighted, to_slot).astype(jnp.bfloat16)]
  transfers between devices with their start and end apart: 1 -> 16, of which waited for: 1 -> 6; matrix products, arithmetic and copies ran while one was open for 21% -> 6% of each run, Pallas kernels for 0% -> 48%
where the time goes in v1:
time: 412 us; the launch traced here: 411 us
  Pallas kernels  198 us (48%)
  waiting for transfers between devices  120 us (29%)
  starting transfers between devices  54.4 us (13%)
  matrix products  21.8 us (5%)
  local copies, waits for them, and re-layouts  11 us (3%)
  other arithmetic  5.01 us (1%)
    ppermute x9, waiting for transfers between devices, shift(): return lax.ppermute(v, 'ep', [(i, i ^ 2 * k) for i in range(n)])  119 us
    pallas_call x4, Pallas kernels, shared_part(): pl.pallas_call(shared_kernel, grid_spec=pltpu.PrefetchScalarGridSpec(num_...  100 us
    pallas_call x2, Pallas kernels, experts_of(): pl.pallas_call(functools.partial(expert_kernel, len(vs)), grid=(mine, ff...  97.7 us
    all_to_all x7, starting transfers between devices, exchange(): return lax.all_to_all(v, 'ep', 0, 0, axis_index_groups=planes, tiled=True)  31 us
    ppermute x9, starting transfers between devices, shift(): return lax.ppermute(v, 'ep', [(i, i ^ 2 * k) for i in range(n)])  23.4 us
    dot_general x8, matrix products, dot(): return jnp.einsum(form, a, b, preferred_element_type=jnp.float32)  21.8 us
  transfers between devices with their start and end apart: 16, of which 6 were waited for; matrix products, arithmetic and copies ran while one was open for 6% of the time, Pallas kernels for 48%

profile of v1, /device:TPU:0, one launch (start us, length us, event | category | flops | bytes accessed | tf_op | source)
XLA Modules:
  0.0 411.4 jit_solution(11053985703058697725)
XLA Ops:
  0.0 0.7 convert_bitcast_fusion
  0.7 0.7 fusion.201
  1.5 3.8 convolution_convert_fusion
  5.4 5.3 %all-to-all-start.4 = ((bf16[8,2,40,1792]{3,2,1,0:T(8,128)(2,1)}), bf16[8,2,40,1792]{3,2,1,0:T(8,128)(2,1)S(1)}, u32[]{:S(2)}, u32[]{:S(2)}) async-start(bf16[8,2,40,1792]{3,2,1,0:T(8,128)(2,1)} %bitcast.99), calls=%async_computation.4 | async-start | bytes 4587520 | tf_op jit(solution)/shard_map/all_to_all | solution.py:137
  10.8 1.6 collective-permute-start.1
  12.4 0.4 collective-permute-start
  12.9 20.9 %collective-permute-done = bf16[24,256]{1,0:T(8,128)(2,1)S(1)} collective-permute-done((bf16[24,256]{1,0:T(8,128)(2,1)S(1)}, bf16[24,256]{1,0:T(8,128)(2,1)S(1)}, u32[]{:S(2)}, u32[]{:S(2)}) %collective-permute-start) | collective-permute-done | bytes 12320 | tf_op jit(solution)/shard_map/ppermute | solution.py:134
  33.9 0.5 copy-done.27
  34.9 2.6 convolution_convert_fusion.3
  37.5 1.1 all-to-all-done.4.refs_1_
  38.6 1.4 copy-done.1
  40.0 4.4 %all-to-all-start = ((bf16[8,2,40,1792]{3,2,1,0:T(8,128)(2,1)}), bf16[8,2,40,1792]{3,2,1,0:T(8,128)(2,1)}, u32[]{:S(2)}, u32[]{:S(2)}) async-start(bf16[8,2,40,1792]{3,2,1,0:T(8,128)(2,1)} %bitcast.97), calls=%async_computation | async-start | bytes 4587520 | tf_op jit(solution)/shard_map/all_to_all | solution.py:137
  44.4 3.7 collective-permute-start.7
  48.3 0.8 collective-permute-start.2
  49.1 2.1 collective-permute-start.3
  51.2 18.6 %collective-permute-done.6 = bf16[24,256]{1,0:T(8,128)(2,1)S(1)} collective-permute-done((bf16[24,256]{1,0:T(8,128)(2,1)S(1)}, bf16[24,256]{1,0:T(8,128)(2,1)S(1)}, u32[]{:S(2)}, u32[]{:S(2)}) %collective-permute-start.6) | collective-permute-done | bytes 12320 | tf_op jit(solution)/shard_map/ppermute | solution.py:134
  70.0 0.5 copy-done.75
  70.9 2.6 convolution_convert_fusion.1
  73.5 4.0 all-to-all-start.3
  77.6 31.5 %collective-permute-done.2 = bf16[24,256]{1,0:T(8,128)(2,1)S(1)} collective-permute-done((bf16[24,256]{1,0:T(8,128)(2,1)S(1)}, bf16[24,256]{1,0:T(8,128)(2,1)S(1)}, u32[]{:S(2)}, u32[]{:S(2)}) %collective-permute-start.2) | collective-permute-done | bytes 12320 | tf_op jit(solution)/shard_map/ppermute | solution.py:134
  109.2 0.6 fusion.208
  109.8 0.6 fusion.209
  110.4 0.6 fusion.212
  111.1 17.1 %collective-permute-done.3.x_ref = bf16[256,1792]{1,0:T(8,128)(2,1)} collective-permute-done((bf16[256,1792]{1,0:T(8,128)(2,1)S(1)}, bf16[256,1792]{1,0:T(8,128)(2,1)}, u32[]{:S(2)}, u32[]{:S(2)}) %collective-permute-start.3) | collective-permute-done | bytes 917536 | tf_op jit(solution)/shard_map/ppermute | solution.py:134
  128.3 3.8 convolution_convert_fusion.2
  132.1 1.4 copy-done.2
  133.5 4.4 %all-to-all-start.1 = ((bf16[8,2,40,1792]{3,2,1,0:T(8,128)(2,1)}), bf16[8,2,40,1792]{3,2,1,0:T(8,128)(2,1)}, u32[]{:S(2)}, u32[]{:S(2)}) async-start(bf16[8,2,40,1792]{3,2,1,0:T(8,128)(2,1)} %bitcast.100), calls=%async_computation.1 | async-start | bytes 4587520 | tf_op jit(solution)/shard_map/all_to_all | solution.py:137
  137.9 48.9 %experts.3 = (bf16[8,2,40,1792]{3,2,1,0:T(8,128)(2,1)}, bf16[8,2,40,1792]{3,2,1,0:T(8,128)(2,1)}) custom-call(bf16[8,2,40,1792]{3,2,1,0:T(8,128)(2,1)} %copy-done.2, bf16[8,2,40,1792]{3,2,1,0:T(8,128)(2,1)} %copy-done.1, bf16[2,1792,2560]{2,1,0:T(8,128)(2,1)} %refs_2_.3, bf16[2,1792,2560]{2,1,0:T(8,128)(2,1)} %refs_3_.3, bf16[2,2560,1792]{2,1,0:T(8,128)(2,1)} %refs_4_.3), custom_call_target="tpu_custom_call" | custom-call | flops 35232153600 | bytes 55050240 | tf_op jit(solution)/shard_map/experts/pallas_call | solution.py:109
  186.8 4.1 all-to-all-start.5
  190.9 48.8 %experts.2 = bf16[8,2,80,1792]{3,2,1,0:T(8,128)(2,1)} custom-call(bf16[8,2,40,1792]{3,2,1,0:T(8,128)(2,1)} %all-to-all-done.refs_0_, bf16[8,2,40,1792]{3,2,1,0:T(8,128)(2,1)} %all-to-all-done.1.refs_1_, bf16[2,1792,2560]{2,1,0:T(8,128)(2,1)} %refs_2_.3, bf16[2,1792,2560]{2,1,0:T(8,128)(2,1)} %refs_3_.3, bf16[2,2560,1792]{2,1,0:T(8,128)(2,1)} %refs_4_.3), custom_call_target="tpu_custom_call" | custom-call | flops 35232153600 | bytes 55050240 | tf_op jit(solution)/shard_map/experts/pallas_call | solution.py:109
  239.7 1.4 copy-done.3
  241.0 4.6 %all-to-all-start.2 = ((bf16[8,2,80,1792]{3,2,1,0:T(8,128)(2,1)}), bf16[8,2,80,1792]{3,2,1,0:T(8,128)(2,1)}, u32[]{:S(2)}, u32[]{:S(2)}) async-start(bf16[8,2,80,1792]{3,2,1,0:T(8,128)(2,1)} %experts.2), calls=%async_computation.2 | async-start | bytes 9175040 | tf_op jit(solution)/shard_map/all_to_all | solution.py:137
  245.7 25.2 %shared.5 = f32[256,1792]{1,0:T(8,128)} custom-call(s32[1]{0:T(128)} %bitcast.z_ref, bf16[256,1792]{1,0:T(8,128)(2,1)} %copy-done.8, bf16[1792,20480]{1,0:T(8,128)(2,1)} %g_ref.7, bf16[1792,20480]{1,0:T(8,128)(2,1)} %u_ref.7, bf16[20480,1792]{1,0:T(8,128)(2,1)} %d_ref.7), custom_call_target="tpu_custom_call" | custom-call | flops 14092861440 | bytes 55050240 | tf_op jit(solution)/shard_map/shared/pallas_call | solution.py:44
  270.9 25.0 %shared.6 = f32[256,1792]{1,0:T(8,128)} custom-call(s32[1]{0:T(128)} %bitcast.z_ref, bf16[256,1792]{1,0:T(8,128)(2,1)} %collective-permute-done.3.x_ref, bf16[1792,20480]{1,0:T(8,128)(2,1)} %g_ref.7, bf16[1792,20480]{1,0:T(8,128)(2,1)} %u_ref.7, bf16[20480,1792]{1,0:T(8,128)(2,1)} %d_ref.7), custom_call_target="tpu_custom_call" | custom-call | flops 14092861440 | bytes 55050240 | tf_op jit(solution)/shard_map/shared/pallas_call | solution.py:44
  296.0 25.0 %shared.7 = f32[256,1792]{1,0:T(8,128)} custom-call(s32[1]{0:T(128)} %bitcast.z_ref, bf16[256,1792]{1,0:T(8,128)(2,1)} %copy-done.9, bf16[1792,20480]{1,0:T(8,128)(2,1)} %g_ref.7, bf16[1792,20480]{1,0:T(8,128)(2,1)} %u_ref.7, bf16[20480,1792]{1,0:T(8,128)(2,1)} %d_ref.7), custom_call_target="tpu_custom_call" | custom-call | flops 14092861440 | bytes 55050240 | tf_op jit(solution)/shard_map/shared/pallas_call | solution.py:44
  321.2 3.5 add_convert_fusion.1
  324.7 2.5 collective-permute-start.8
  327.2 4.2 %all-to-all-start.6 = ((bf16[8,2,40,1792]{3,2,1,0:T(8,128)(2,1)}), bf16[8,2,40,1792]{3,2,1,0:T(8,128)(2,1)S(1)}, u32[]{:S(2)}, u32[]{:S(2)}) async-start(bf16[8,2,40,1792]{3,2,1,0:T(8,128)(2,1)} %get-tuple-element.8), calls=%async_computation.6 | async-start | bytes 4587520 | tf_op jit(solution)/shard_map/all_to_all | solution.py:137
  331.5 2.7 fusion.207
  334.6 2.1 add_convert_fusion.3
  336.7 11.3 %collective-permute-start.4 = (bf16[256,1792]{1,0:T(8,128)(2,1)}, bf16[256,1792]{1,0:T(8,128)(2,1)}, u32[]{:S(2)}, u32[]{:S(2)}) collective-permute-start(bf16[256,1792]{1,0:T(8,128)(2,1)} %add_convert_fusion.3), channel_id=1, source_target_pairs={{0,2},{1,3},{2,0},{3,1},{4,6},{5,7},{6,4},{7,5},{8,10},{9,11},{10,... | collective-permute-start | bytes 2752520 | tf_op jit(solution)/shard_map/ppermute | solution.py:134
  348.1 2.1 add_convert_fusion.2
  350.3 0.7 collective-permute-start.5
  351.0 24.9 %shared.4 = f32[256,1792]{1,0:T(8,128)} custom-call(s32[1]{0:T(128)} %bitcast.z_ref, bf16[256,1792]{1,0:T(8,128)(2,1)} %bitcast.101, bf16[1792,20480]{1,0:T(8,128)(2,1)} %g_ref.7, bf16[1792,20480]{1,0:T(8,128)(2,1)} %u_ref.7, bf16[20480,1792]{1,0:T(8,128)(2,1)} %d_ref.7), custom_call_target="tpu_custom_call" | custom-call | flops 14092861440 | bytes 55050240 | tf_op jit(solution)/shard_map/shared/pallas_call | solution.py:44
  375.9 0.7 slice_convert_fusion
  376.7 1.1 fusion.36
  377.9 30.7 %collective-permute-done.5 = bf16[256,1792]{1,0:T(8,128)(2,1)} collective-permute-done((bf16[256,1792]{1,0:T(8,128)(2,1)}, bf16[256,1792]{1,0:T(8,128)(2,1)}, u32[]{:S(2)}, u32[]{:S(2)}) %collective-permute-start.5) | collective-permute-done | bytes 917536 | tf_op jit(solution)/shard_map/ppermute | solution.py:134
  408.5 2.8 fusion
  (217 shorter events, 1.6 us)
Async XLA Ops:
  1.4 46.9 %copy-start.10 = (bf16[24,256]{1,0:T(8,128)(2,1)}, bf16[24,256]{1,0:T(8,128)(2,1)S(1)}, u32[]{:S(2)}) copy-start(bf16[24,256]{1,0:T(8,128)(2,1)S(1)} %maximum_bitcast_fusion) | copy-start | bytes 36868
  5.4 33.2 %all-to-all-start.4 = ((bf16[8,2,40,1792]{3,2,1,0:T(8,128)(2,1)}), bf16[8,2,40,1792]{3,2,1,0:T(8,128)(2,1)S(1)}, u32[]{:S(2)}, u32[]{:S(2)}) async-start(bf16[8,2,40,1792]{3,2,1,0:T(8,128)(2,1)} %bitcast.99), calls=%async_computation.4 | async-start | bytes 4587520 | tf_op jit(solution)/shard_map/all_to_all | solution.py:137
  10.8 23.1 %collective-permute-start.1 = (bf16[256,1792]{1,0:T(8,128)(2,1)S(1)}, bf16[256,1792]{1,0:T(8,128)(2,1)S(1)}, u32[]{:S(2)}, u32[]{:S(2)}) collective-permute-start(bf16[256,1792]{1,0:T(8,128)(2,1)S(1)} %bitcast.102), channel_id=1, source_target_pairs={{0,2},{1,3},{2,0},{3,1},{4,6},{5,7},{6,4},{7,5},{8,10},{9,11},{10,... | collective-permute-start | bytes 2752520 | tf_op jit(solution)/shard_map/ppermute | solution.py:134
  12.4 21.4 %collective-permute-start = (bf16[24,256]{1,0:T(8,128)(2,1)S(1)}, bf16[24,256]{1,0:T(8,128)(2,1)S(1)}, u32[]{:S(2)}, u32[]{:S(2)}) collective-permute-start(bf16[24,256]{1,0:T(8,128)(2,1)S(1)} %maximum_bitcast_fusion), channel_id=1, source_target_pairs={{0,2},{1,3},{2,0},{3,1},{4,6},{5,7},{6,4},{7,5},{8,10},{9,11},{10,... | collective-permute-start | bytes 36872 | tf_op jit(solution)/shard_map/ppermute | solution.py:134
  40.0 33.5 %all-to-all-start = ((bf16[8,2,40,1792]{3,2,1,0:T(8,128)(2,1)}), bf16[8,2,40,1792]{3,2,1,0:T(8,128)(2,1)}, u32[]{:S(2)}, u32[]{:S(2)}) async-start(bf16[8,2,40,1792]{3,2,1,0:T(8,128)(2,1)} %bitcast.97), calls=%async_computation | async-start | bytes 4587520 | tf_op jit(solution)/shard_map/all_to_all | solution.py:137
  44.4 25.6 %collective-permute-start.7 = (bf16[256,1792]{1,0:T(8,128)(2,1)S(1)}, bf16[256,1792]{1,0:T(8,128)(2,1)S(1)}, u32[]{:S(2)}, u32[]{:S(2)}) collective-permute-start(bf16[256,1792]{1,0:T(8,128)(2,1)S(1)} %bitcast.103), channel_id=1, source_target_pairs={{0,6},{1,7},{2,4},{3,5},{4,2},{5,3},{6,0},{7,1},{8,14},{9,15},{10,... | collective-permute-start | bytes 2752520 | tf_op jit(solution)/shard_map/ppermute | solution.py:134
  48.1 21.8 %collective-permute-start.6 = (bf16[24,256]{1,0:T(8,128)(2,1)S(1)}, bf16[24,256]{1,0:T(8,128)(2,1)S(1)}, u32[]{:S(2)}, u32[]{:S(2)}) collective-permute-start(bf16[24,256]{1,0:T(8,128)(2,1)S(1)} %maximum_bitcast_fusion), channel_id=1, source_target_pairs={{0,6},{1,7},{2,4},{3,5},{4,2},{5,3},{6,0},{7,1},{8,14},{9,15},{10,... | collective-permute-start | bytes 36872 | tf_op jit(solution)/shard_map/ppermute | solution.py:134
  48.3 60.8 %collective-permute-start.2 = (bf16[24,256]{1,0:T(8,128)(2,1)S(1)}, bf16[24,256]{1,0:T(8,128)(2,1)S(1)}, u32[]{:S(2)}, u32[]{:S(2)}) collective-permute-start(bf16[24,256]{1,0:T(8,128)(2,1)S(1)} %maximum_bitcast_fusion), channel_id=1, source_target_pairs={{0,4},{1,5},{2,6},{3,7},{4,0},{5,1},{6,2},{7,3},{8,12},{9,13},{10,... | collective-permute-start | bytes 36872 | tf_op jit(solution)/shard_map/ppermute | solution.py:134
  49.1 79.1 %collective-permute-start.3 = (bf16[256,1792]{1,0:T(8,128)(2,1)S(1)}, bf16[256,1792]{1,0:T(8,128)(2,1)}, u32[]{:S(2)}, u32[]{:S(2)}) collective-permute-start(bf16[256,1792]{1,0:T(8,128)(2,1)S(1)} %bitcast.104), channel_id=1, source_target_pairs={{0,4},{1,5},{2,6},{3,7},{4,0},{5,1},{6,2},{7,3},{8,12},{9,13},{10,... | collective-permute-start | bytes 2752520 | tf_op jit(solution)/shard_map/ppermute | solution.py:134
  73.5 58.5 %all-to-all-start.3 = ((bf16[8,2,40,1792]{3,2,1,0:T(8,128)(2,1)}), bf16[8,2,40,1792]{3,2,1,0:T(8,128)(2,1)S(1)}, u32[]{:S(2)}, u32[]{:S(2)}) async-start(bf16[8,2,40,1792]{3,2,1,0:T(8,128)(2,1)} %bitcast.96), calls=%async_computation.3 | async-start | bytes 4587520 | tf_op jit(solution)/shard_map/all_to_all | solution.py:137
  109.1 19.1 %copy-start.43 = (s32[1,256]{1,0:T(1,128)}, s32[1,256]{1,0:T(1,128)S(1)}, u32[]{:S(2)}) copy-start(s32[1,256]{1,0:T(1,128)S(1)} %get-tuple-element.27) | copy-start | bytes 3076
  109.1 19.0 %copy-start.45 = (s32[1,256]{1,0:T(1,128)}, s32[1,256]{1,0:T(1,128)S(1)}, u32[]{:S(2)}) copy-start(s32[1,256]{1,0:T(1,128)S(1)} %get-tuple-element.28) | copy-start | bytes 3076
  109.2 19.0 %copy-start.47 = (s32[1,256]{1,0:T(1,128)}, s32[1,256]{1,0:T(1,128)S(1)}, u32[]{:S(2)}) copy-start(s32[1,256]{1,0:T(1,128)S(1)} %get-tuple-element.29) | copy-start | bytes 3076
  109.2 19.0 %copy-start.49 = (s32[1,256]{1,0:T(1,128)}, s32[1,256]{1,0:T(1,128)S(1)}, u32[]{:S(2)}) copy-start(s32[1,256]{1,0:T(1,128)S(1)} %get-tuple-element.30) | copy-start | bytes 3076
  109.2 19.0 %copy-start.51 = (s32[1,256]{1,0:T(1,128)}, s32[1,256]{1,0:T(1,128)S(1)}, u32[]{:S(2)}) copy-start(s32[1,256]{1,0:T(1,128)S(1)} %get-tuple-element.31) | copy-start | bytes 3076
  133.5 53.3 %all-to-all-start.1 = ((bf16[8,2,40,1792]{3,2,1,0:T(8,128)(2,1)}), bf16[8,2,40,1792]{3,2,1,0:T(8,128)(2,1)}, u32[]{:S(2)}, u32[]{:S(2)}) async-start(bf16[8,2,40,1792]{3,2,1,0:T(8,128)(2,1)} %bitcast.100), calls=%async_computation.1 | async-start | bytes 4587520 | tf_op jit(solution)/shard_map/all_to_all | solution.py:137
  186.8 52.9 %all-to-all-start.5 = ((bf16[8,2,40,1792]{3,2,1,0:T(8,128)(2,1)}), bf16[8,2,40,1792]{3,2,1,0:T(8,128)(2,1)S(1)}, u32[]{:S(2)}, u32[]{:S(2)}) async-start(bf16[8,2,40,1792]{3,2,1,0:T(8,128)(2,1)} %get-tuple-element.7), calls=%async_computation.5 | async-start | bytes 4587520 | tf_op jit(solution)/shard_map/all_to_all | solution.py:137
  241.0 86.1 %all-to-all-start.2 = ((bf16[8,2,80,1792]{3,2,1,0:T(8,128)(2,1)}), bf16[8,2,80,1792]{3,2,1,0:T(8,128)(2,1)}, u32[]{:S(2)}, u32[]{:S(2)}) async-start(bf16[8,2,80,1792]{3,2,1,0:T(8,128)(2,1)} %experts.2), calls=%async_computation.2 | async-start | bytes 9175040 | tf_op jit(solution)/shard_map/all_to_all | solution.py:137
  295.9 25.1 %copy-start.4 = (bf16[8,2,40,1792]{3,2,1,0:T(8,128)(2,1)S(1)}, bf16[8,2,40,1792]{3,2,1,0:T(8,128)(2,1)}, u32[]{:S(2)}) copy-start(bf16[8,2,40,1792]{3,2,1,0:T(8,128)(2,1)} %copy-done.3) | copy-start | bytes 6881284
  295.9 25.1 %copy-start.76 = (s32[1,256]{1,0:T(1,128)S(1)}, s32[1,256]{1,0:T(1,128)}, u32[]{:S(2)}) copy-start(s32[1,256]{1,0:T(1,128)} %copy-done.75) | copy-start | bytes 3076
  295.9 25.1 %copy-start.78 = (s32[1,256]{1,0:T(1,128)S(1)}, s32[1,256]{1,0:T(1,128)}, u32[]{:S(2)}) copy-start(s32[1,256]{1,0:T(1,128)} %copy-done.77) | copy-start | bytes 3076
  295.9 25.1 %copy-start.80 = (s32[1,256]{1,0:T(1,128)S(1)}, s32[1,256]{1,0:T(1,128)}, u32[]{:S(2)}) copy-start(s32[1,256]{1,0:T(1,128)} %copy-done.79) | copy-start | bytes 3076
  295.9 25.1 %copy-start.82 = (s32[1,256]{1,0:T(1,128)S(1)}, s32[1,256]{1,0:T(1,128)}, u32[]{:S(2)}) copy-start(s32[1,256]{1,0:T(1,128)} %copy-done.81) | copy-start | bytes 3076
  295.9 25.1 %copy-start.84 = (s32[1,256]{1,0:T(1,128)S(1)}, s32[1,256]{1,0:T(1,128)}, u32[]{:S(2)}) copy-start(s32[1,256]{1,0:T(1,128)} %copy-done.83) | copy-start | bytes 3076
  295.9 25.1 %copy-start.86 = (s32[1,256]{1,0:T(1,128)S(1)}, s32[1,256]{1,0:T(1,128)}, u32[]{:S(2)}) copy-start(s32[1,256]{1,0:T(1,128)} %copy-done.85) | copy-start | bytes 3076
  295.9 25.1 %copy-start.88 = (s32[1,256]{1,0:T(1,128)S(1)}, s32[1,256]{1,0:T(1,128)}, u32[]{:S(2)}) copy-start(s32[1,256]{1,0:T(1,128)} %copy-done.87) | copy-start | bytes 3076
  295.9 25.1 %copy-start.90 = (s32[1,256]{1,0:T(1,128)S(1)}, s32[1,256]{1,0:T(1,128)}, u32[]{:S(2)}) copy-start(s32[1,256]{1,0:T(1,128)} %copy-done.89) | copy-start | bytes 3076
  296.0 25.1 %copy-start.91 = (f32[1,256]{1,0:T(1,128)S(1)}, f32[1,256]{1,0:T(1,128)}, u32[]{:S(2)}) copy-start(f32[1,256]{1,0:T(1,128)} %get-tuple-element.43) | copy-start | bytes 3076
  296.0 25.1 %copy-start.92 = (f32[1,256]{1,0:T(1,128)S(1)}, f32[1,256]{1,0:T(1,128)}, u32[]{:S(2)}) copy-start(f32[1,256]{1,0:T(1,128)} %get-tuple-element.44) | copy-start | bytes 3076
  296.0 25.1 %copy-start.93 = (f32[1,256]{1,0:T(1,128)S(1)}, f32[1,256]{1,0:T(1,128)}, u32[]{:S(2)}) copy-start(f32[1,256]{1,0:T(1,128)} %get-tuple-element.45) | copy-start | bytes 3076
  296.0 25.1 %copy-start.94 = (f32[1,256]{1,0:T(1,128)S(1)}, f32[1,256]{1,0:T(1,128)}, u32[]{:S(2)}) copy-start(f32[1,256]{1,0:T(1,128)} %get-tuple-element.46) | copy-start | bytes 3076
  296.0 25.1 %copy-start.95 = (f32[1,256]{1,0:T(1,128)S(1)}, f32[1,256]{1,0:T(1,128)}, u32[]{:S(2)}) copy-start(f32[1,256]{1,0:T(1,128)} %get-tuple-element.47) | copy-start | bytes 3076
  296.0 25.1 %copy-start.96 = (f32[1,256]{1,0:T(1,128)S(1)}, f32[1,256]{1,0:T(1,128)}, u32[]{:S(2)}) copy-start(f32[1,256]{1,0:T(1,128)} %get-tuple-element.48) | copy-start | bytes 3076
  296.0 25.1 %copy-start.97 = (f32[1,256]{1,0:T(1,128)S(1)}, f32[1,256]{1,0:T(1,128)}, u32[]{:S(2)}) copy-start(f32[1,256]{1,0:T(1,128)} %get-tuple-element.49) | copy-start | bytes 3076
  296.0 25.1 %copy-start.98 = (f32[1,256]{1,0:T(1,128)S(1)}, f32[1,256]{1,0:T(1,128)}, u32[]{:S(2)}) copy-start(f32[1,256]{1,0:T(1,128)} %get-tuple-element.50) | copy-start | bytes 3076
  324.7 53.1 %collective-permute-start.8 = (bf16[256,1792]{1,0:T(8,128)(2,1)}, bf16[256,1792]{1,0:T(8,128)(2,1)S(1)}, u32[]{:S(2)}, u32[]{:S(2)}) collective-permute-start(bf16[256,1792]{1,0:T(8,128)(2,1)} %add_convert_fusion.1), channel_id=1, source_target_pairs={{0,6},{1,7},{2,4},{3,5},{4,2},{5,3},{6,0},{7,1},{8,14},{9,15},{10,... | collective-permute-start | bytes 2752520 | tf_op jit(solution)/shard_map/ppermute | solution.py:134
  327.2 49.5 %all-to-all-start.6 = ((bf16[8,2,40,1792]{3,2,1,0:T(8,128)(2,1)}), bf16[8,2,40,1792]{3,2,1,0:T(8,128)(2,1)S(1)}, u32[]{:S(2)}, u32[]{:S(2)}) async-start(bf16[8,2,40,1792]{3,2,1,0:T(8,128)(2,1)} %get-tuple-element.8), calls=%async_computation.6 | async-start | bytes 4587520 | tf_op jit(solution)/shard_map/all_to_all | solution.py:137
  336.7 41.2 %collective-permute-start.4 = (bf16[256,1792]{1,0:T(8,128)(2,1)}, bf16[256,1792]{1,0:T(8,128)(2,1)}, u32[]{:S(2)}, u32[]{:S(2)}) collective-permute-start(bf16[256,1792]{1,0:T(8,128)(2,1)} %add_convert_fusion.3), channel_id=1, source_target_pairs={{0,2},{1,3},{2,0},{3,1},{4,6},{5,7},{6,4},{7,5},{8,10},{9,11},{10,... | collective-permute-start | bytes 2752520 | tf_op jit(solution)/shard_map/ppermute | solution.py:134
  350.2 26.4 %copy-start.12 = (s32[1,256]{1,0:T(1,128)S(1)}, s32[1,256]{1,0:T(1,128)}, u32[]{:S(2)}) copy-start(s32[1,256]{1,0:T(1,128)} %copy-done.11) | copy-start | bytes 3076
  350.2 26.4 %copy-start.14 = (s32[1,256]{1,0:T(1,128)S(1)}, s32[1,256]{1,0:T(1,128)}, u32[]{:S(2)}) copy-start(s32[1,256]{1,0:T(1,128)} %copy-done.13) | copy-start | bytes 3076
  350.2 26.4 %copy-start.16 = (s32[1,256]{1,0:T(1,128)S(1)}, s32[1,256]{1,0:T(1,128)}, u32[]{:S(2)}) copy-start(s32[1,256]{1,0:T(1,128)} %copy-done.15) | copy-start | bytes 3076
  350.2 26.5 %copy-start.18 = (s32[1,256]{1,0:T(1,128)S(1)}, s32[1,256]{1,0:T(1,128)}, u32[]{:S(2)}) copy-start(s32[1,256]{1,0:T(1,128)} %copy-done.17) | copy-start | bytes 3076
  350.2 26.5 %copy-start.20 = (s32[1,256]{1,0:T(1,128)S(1)}, s32[1,256]{1,0:T(1,128)}, u32[]{:S(2)}) copy-start(s32[1,256]{1,0:T(1,128)} %copy-done.19) | copy-start | bytes 3076
  350.2 26.5 %copy-start.22 = (s32[1,256]{1,0:T(1,128)S(1)}, s32[1,256]{1,0:T(1,128)}, u32[]{:S(2)}) copy-start(s32[1,256]{1,0:T(1,128)} %copy-done.21) | copy-start | bytes 3076
  350.3 26.5 %copy-start.24 = (s32[1,256]{1,0:T(1,128)S(1)}, s32[1,256]{1,0:T(1,128)}, u32[]{:S(2)}) copy-start(s32[1,256]{1,0:T(1,128)} %copy-done.23) | copy-start | bytes 3076
  350.3 26.5 %copy-start.26 = (s32[1,256]{1,0:T(1,128)S(1)}, s32[1,256]{1,0:T(1,128)}, u32[]{:S(2)}) copy-start(s32[1,256]{1,0:T(1,128)} %copy-done.25) | copy-start | bytes 3076
  350.3 58.3 %collective-permute-start.5 = (bf16[256,1792]{1,0:T(8,128)(2,1)}, bf16[256,1792]{1,0:T(8,128)(2,1)}, u32[]{:S(2)}, u32[]{:S(2)}) collective-permute-start(bf16[256,1792]{1,0:T(8,128)(2,1)} %add_convert_fusion.2), channel_id=1, source_target_pairs={{0,4},{1,5},{2,6},{3,7},{4,0},{5,1},{6,2},{7,3},{8,12},{9,13},{10,... | collective-permute-start | bytes 2752520 | tf_op jit(solution)/shard_map/ppermute | solution.py:134
  376.7 31.8 %copy-start = (f32[256,1792]{1,0:T(8,128)S(1)}, f32[256,1792]{1,0:T(8,128)}, u32[]{:S(2)}) copy-start(f32[256,1792]{1,0:T(8,128)} %shared.4) | copy-start | bytes 5505028
  (67 other events, 388.7 us)

commit v2 on v1

v2 whole, which is shorter than its diff:
```python
import functools

import jax
import jax.numpy as jnp
from jax import lax
from jax.experimental import pallas as pl
from jax.experimental.pallas import tpu as pltpu
from jax.sharding import PartitionSpec as P


ZS = 4
PLANE = 8
PAIRS = ((1, 2), (3, 0))
BACK = ((1, 2), (3,), (0,))
SHARED_TILE = 1024
EXPERT_TILE = 512
DOWN_TILE = 256
SHARED_SPLIT = (0, 5, 9, 13, 16, 20)
VMEM = 67043328


def mm(a, b):
    return jnp.dot(a, b, preferred_element_type=jnp.float32)


def rows_of(route, z, mine, slots):
    top = route.shape[0] // 3
    e, s = route[:top].astype(jnp.int32), route[top : 2 * top].astype(jnp.int32)
    d, i = e >> 1, e & 1
    p = ((d >> 4) << 2) | (((d >> 3) & 1) << 1) | (d & 1)
    return jnp.where((((d >> 1) & (ZS - 1)) == z) & (s < slots), (p * mine + i) * slots + s, -1)


def select_kernel(z_ref, route_ref, x_ref, o_ref):
    senders, mine, slots, _ = o_ref.shape
    count = senders * mine * slots
    row = rows_of(route_ref[...].astype(jnp.float32), z_ref[0], mine, slots)
    here = lax.broadcasted_iota(jnp.int32, (count, row.shape[1]), 0) + pl.program_id(0) * count
    pick = here == row[0:1]
    for j in range(1, row.shape[0]):
        pick = pick | (here == row[j : j + 1])
    pick = jnp.where(pick, 1.0, 0.0).astype(jnp.bfloat16)
    o_ref[...] = mm(pick, x_ref[...]).astype(o_ref.dtype).reshape(o_ref.shape)


def select(z, route, x, mine, slots):
    tokens, d = x.shape
    step = 4
    return pl.pallas_call(
        select_kernel,
        grid_spec=pltpu.PrefetchScalarGridSpec(
            num_scalar_prefetch=1,
            grid=(PLANE // step,),
            in_specs=[
                pl.BlockSpec(route.shape, lambda i, z: (0, 0)),
                pl.BlockSpec((tokens, d), lambda i, z: (0, 0)),
            ],
            out_specs=pl.BlockSpec((step, mine, slots, d), lambda i, z: (i, 0, 0, 0)),
        ),
        out_shape=pltpu.HBM((PLANE, mine, slots, d), jnp.bfloat16),
        compiler_params=pltpu.CompilerParams(vmem_limit_bytes=VMEM, dimension_semantics=("arbitrary",)),
        cost_estimate=pl.CostEstimate(
            flops=2 * PLANE * mine * slots * tokens * d, bytes_accessed=2 * d * (tokens + PLANE * mine * slots), transcendentals=0
        ),
        name="select",
    )(z.reshape(1), route, x)


def combine_kernel(parts, extra, z_ref, v_ref, *refs):
    routes, adds = refs[:parts], refs[parts : parts + extra]
    outs, weight = refs[parts + extra : -1], refs[-1]
    senders, mine, wide, tile = v_ref.shape
    slots = wide // parts
    rows = senders * mine * slots

    @pl.when(pl.program_id(0) == 0)
    def _():
        for j in range(parts):
            route = routes[j][...].astype(jnp.float32)
            row = rows_of(route, z_ref[0], mine, slots)
            top = row.shape[0]
            here = lax.broadcasted_iota(jnp.int32, (rows, row.shape[1]), 0)
            w = jnp.zeros(here.shape, jnp.float32)
            for i in range(top):
                w = jnp.where(here == row[i : i + 1], route[2 * top + i : 2 * top + i + 1], w)
            weight[j] = w.astype(jnp.bfloat16)

    for j in range(parts):
        v = v_ref[:, :, pl.ds(j * slots, slots), :].reshape(rows, tile)
        y = lax.dot_general(weight[j], v, (((0,), (0,)), ((), ())), preferred_element_type=jnp.float32)
        for add in adds:
            y = y + add[...].astype(jnp.float32)
        outs[j][...] = y.astype(jnp.bfloat16)


def combine(z, v, routes, adds):
    parts = len(routes)
    senders, mine, wide, d = v.shape
    tokens = routes[0].shape[1]
    tile = d // 2
    flat = pl.BlockSpec((tokens, tile), lambda i, z: (0, i))
    return pl.pallas_call(
        functools.partial(combine_kernel, parts, len(adds)),
        grid_spec=pltpu.PrefetchScalarGridSpec(
            num_scalar_prefetch=1,
            grid=(d // tile,),
            in_specs=[pl.BlockSpec((senders, mine, wide, tile), lambda i, z: (0, 0, 0, i))]
            + [pl.BlockSpec(routes[0].shape, lambda i, z: (0, 0))] * parts
            + [flat] * len(adds),
            out_specs=[flat] * parts,
            scratch_shapes=[pltpu.VMEM((parts, senders * mine * wide // parts, tokens), jnp.bfloat16)],
        ),
        out_shape=[jax.ShapeDtypeStruct((tokens, d), jnp.bfloat16)] * parts,
        compiler_params=pltpu.CompilerParams(vmem_limit_bytes=VMEM, dimension_semantics=("arbitrary",)),
        cost_estimate=pl.CostEstimate(
            flops=2 * senders * mine * wide * tokens * d, bytes_accessed=2 * d * senders * mine * wide, transcendentals=0
        ),
        name="combine",
    )(z.reshape(1), v, *routes, *adds)


def shared_kernel(started, x_ref, g_ref, u_ref, d_ref, *refs):
    o_ref = refs[-1]
    h = (jax.nn.silu(mm(x_ref[...], g_ref[...])) * mm(x_ref[...], u_ref[...])).astype(jnp.bfloat16)

    @pl.when(pl.program_id(0) == 0)
    def _():
        o_ref[...] = refs[0][...] if started else jnp.zeros_like(o_ref)

    o_ref[...] += mm(h, d_ref[...])


def shared_part(x, s_gate, s_up, s_down, first, last, total):
    rows, d = x.shape
    tile, steps = SHARED_TILE, last - first
    whole = pl.BlockSpec((rows, d), lambda i: (0, 0))
    return pl.pallas_call(
        functools.partial(shared_kernel, total is not None),
        grid=(steps,),
        in_specs=[
            whole,
            pl.BlockSpec((d, tile), lambda i: (0, i + first)),
            pl.BlockSpec((d, tile), lambda i: (0, i + first)),
            pl.BlockSpec((tile, d), lambda i: (i + first, 0)),
        ]
        + [whole] * (total is not None),
        out_specs=whole,
        out_shape=jax.ShapeDtypeStruct((rows, d), jnp.float32),
        compiler_params=pltpu.CompilerParams(vmem_limit_bytes=VMEM, dimension_semantics=("arbitrary",)),
        cost_estimate=pl.CostEstimate(
            flops=6 * rows * d * tile * steps, bytes_accessed=6 * d * tile * steps, transcendentals=rows * tile * steps
        ),
        name="shared",
    )(x, s_gate, s_up, s_down, *([] if total is None else [total]))


def expert_kernel(count, *refs):
    v_refs, (g_ref, u_ref, d_hbm), o_refs = refs[:count], refs[count : count + 3], refs[count + 3 : -4]
    held, h, down, sem = refs[-4:]
    d = held.shape[-1]
    part = held.shape[0] // count
    tile = g_ref.shape[-1]
    e, f = pl.program_id(0), pl.program_id(1)
    fetch = pltpu.make_async_copy(d_hbm.at[e], down, sem)

    @pl.when(f == 0)
    def _():
        fetch.start()
        for j, v_ref in enumerate(v_refs):
            held[pl.ds(j * part, part)] = v_ref[...].reshape(part, d)

    v = held[...]
    out = (jax.nn.silu(mm(v, g_ref[0])) * mm(v, u_ref[0])).astype(jnp.bfloat16)
    h[:, pl.ds(pl.multiple_of(f * tile, tile), tile)] = out

    @pl.when(f == pl.num_programs(1) - 1)
    def _():
        fetch.wait()
        shape = v_refs[0].shape[:-1]
        for c in range(0, d, DOWN_TILE):
            columns = pl.ds(c, DOWN_TILE)
            y = mm(h[...], down[:, columns]).astype(jnp.bfloat16)
            for j in range(count):
                piece = y[j * part : (j + 1) * part].reshape(*shape, DOWN_TILE)
                if len(o_refs) == 1:
                    o_refs[0][:, :, pl.ds(j * shape[2], shape[2]), columns] = piece
                else:
                    o_refs[j][:, :, :, columns] = piece


def experts_of(vs, w_gate, w_up, w_down, joined):
    senders, mine, slots, d = vs[0].shape
    rows = len(vs) * senders * slots
    ff = w_gate.shape[-1]
    tile = EXPERT_TILE
    block = pl.BlockSpec((senders, 1, slots, d), lambda e, f: (0, e, 0, 0))
    outs = 1 if joined else len(vs)
    wide = slots * len(vs) // outs
    return pl.pallas_call(
        functools.partial(expert_kernel, len(vs)),
        grid=(mine, ff // tile),
        in_specs=[block] * len(vs)
        + [
            pl.BlockSpec((1, d, tile), lambda e, f: (e, 0, f)),
            pl.BlockSpec((1, d, tile), lambda e, f: (e, 0, f)),
            pl.BlockSpec(memory_space=pl.ANY),
        ],
        out_specs=[pl.BlockSpec((senders, 1, wide, d), lambda e, f: (0, e, 0, 0))] * outs,
        out_shape=[pltpu.HBM((senders, mine, wide, d), jnp.bfloat16)] * outs,
        scratch_shapes=[
            pltpu.VMEM((rows, d), jnp.bfloat16),
            pltpu.VMEM((rows, ff), jnp.bfloat16),
            pltpu.VMEM((ff, d), jnp.bfloat16),
            pltpu.SemaphoreType.DMA,
        ],
        compiler_params=pltpu.CompilerParams(vmem_limit_bytes=VMEM, dimension_semantics=("arbitrary", "arbitrary")),
        cost_estimate=pl.CostEstimate(
            flops=6 * mine * rows * d * ff, bytes_accessed=6 * mine * d * ff, transcendentals=mine * rows * ff
        ),
        name="experts",
    )(*vs, w_gate, w_up, w_down)


def solution(mesh):
    n = mesh.shape["ep"]
    planes = [[16 * x + 8 * y + 2 * z + c for x in (0, 1) for y in (0, 1) for c in (0, 1)] for z in range(ZS)]

    def shift(v, k):
        return lax.ppermute(v, "ep", [(i, i ^ (2 * k)) for i in range(n)])

    def exchange(v):
        return lax.all_to_all(v, "ep", 0, 0, axis_index_groups=planes, tiled=True)

    def body(x, expert, slot, gate, w_gate, w_up, w_down, s_gate, s_up, s_down):
        x, expert, slot, gate = x[0, 0], expert[0, 0], slot[0, 0], gate[0, 0]
        tokens, top = expert.shape
        mine = w_gate.shape[0]
        slots = 5 * tokens * top // (4 * mine * n)
        z = (lax.axis_index("ep") >> 1) & (ZS - 1)

        route = jnp.concatenate([expert, jnp.minimum(slot, slots)], 1).astype(jnp.bfloat16)
        route = jnp.concatenate([route, gate.astype(jnp.bfloat16)], 1).T
        routes, xs = [route], [x]
        for k in range(1, ZS):
            routes.append(shift(route, k))
            xs.append(shift(x, k))

        sent = []
        for k in range(ZS):
            sent.append(select(z, routes[k], xs[k], mine, slots))
        got = [exchange(v) for v in sent]
        outs = []
        for i, pair in enumerate(PAIRS):
            outs += experts_of([got[k] for k in pair], w_gate, w_up, w_down, joined=i == 0)

        shared = None
        for first, last in zip(SHARED_SPLIT, SHARED_SPLIT[1:]):
            shared = shared_part(x, s_gate, s_up, s_down, first, last, shared)

        arrived = []
        for i, group in enumerate(BACK):
            v = exchange(outs[i])
            parts = combine(z, v, [routes[k] for k in group], () if any(group) else (shared, *arrived))
            for k, part in zip(group, parts):
                if k:
                    arrived.append(shift(part, k))
        return parts[0][None, None]

    tok, exp, rep = P("dp", "ep"), P("ep"), P()

    return jax.shard_map(
        body,
        mesh=mesh,
        in_specs=(tok, tok, tok, tok, exp, exp, exp, rep, rep, rep),
        out_specs=tok,
        check_vma=False,
    )
```

time: 412 us -> 428 us (1.039)
  Pallas kernels: 198 us -> 228 us
  matrix products: 21.8 us -> 0 us
  waiting for transfers between devices: 120 us -> 131 us
  starting transfers between devices: 54.4 us -> 64.1 us
  local copies, waits for them, and re-layouts: 11 us -> 1.81 us
    pallas_call x4 -> x12, Pallas kernels: 100 us -> 140 us  [the longest x5 111 us: shared_part(): pl.pallas_call(functools.partial(shared_kernel, total is not None), grid=...]
    dot_general x8 -> x0, matrix products: 21.8 us -> none  [dot(): return jnp.einsum(form, a, b, preferred_element_type=jnp.float32)]
    ppermute x9, waiting for transfers between devices: 119 us -> 131 us  [shift(): return lax.ppermute(v, 'ep', [(i, i ^ 2 * k) for i in range(n)])]
    pallas_call x2, Pallas kernels: 97.7 us -> 88 us  [experts_of(): pl.pallas_call(functools.partial(expert_kernel, len(vs)), grid=(mine, ff...]
    ppermute x9, starting transfers between devices: 23.4 us -> 31.8 us  [shift(): return lax.ppermute(v, 'ep', [(i, i ^ 2 * k) for i in range(n)])]
    slice x9 -> x0, local copies, waits for them, and re-layouts: 4.64 us -> none  [the longest x1 2.74 us: body(): back = v[:, :, j * slots:(j + 1) * slots].reshape(rows, -1)]
    unnamed x198 -> x18, local copies, waits for them, and re-layouts: 6.37 us -> 1.81 us
  transfers between devices with their start and end apart: 16 -> 16, of which waited for: 6 -> 6; matrix products, arithmetic and copies ran while one was open for 6% -> 0% of each run, Pallas kernels for 48% -> 51%
where the time goes in v2:
time: 428 us; the launch traced here: 427 us
  Pallas kernels  228 us (53%)
  waiting for transfers between devices  131 us (31%)
  starting transfers between devices  64.1 us (15%)
    ppermute x9, waiting for transfers between devices, shift(): return lax.ppermute(v, 'ep', [(i, i ^ 2 * k) for i in range(n)])  131 us
    pallas_call x5, Pallas kernels, shared_part(): pl.pallas_call(functools.partial(shared_kernel, total is not None), grid=...  111 us
    pallas_call x2, Pallas kernels, experts_of(): pl.pallas_call(functools.partial(expert_kernel, len(vs)), grid=(mine, ff...  88 us
    all_to_all x7, starting transfers between devices, exchange(): return lax.all_to_all(v, 'ep', 0, 0, axis_index_groups=planes, tiled=True)  32.3 us
    ppermute x9, starting transfers between devices, shift(): return lax.ppermute(v, 'ep', [(i, i ^ 2 * k) for i in range(n)])  31.8 us
    pallas_call x4, Pallas kernels, select(): pl.pallas_call(select_kernel, grid_spec=pltpu.PrefetchScalarGridSpec(num_...  14.6 us
    pallas_call x3, Pallas kernels, combine(): pl.pallas_call(functools.partial(combine_kernel, parts, len(adds)), grid_...  13.6 us
  transfers between devices with their start and end apart: 16, of which 6 were waited for; matrix products, arithmetic and copies ran while one was open for 0% of the time, Pallas kernels for 51%

profile of v2, /device:TPU:0, one launch (start us, length us, event | category | flops | bytes accessed | tf_op | source)
XLA Modules:
  0.0 427.1 jit_solution(170426408894422691)
XLA Ops:
  0.0 0.7 convert_bitcast_fusion
  0.7 0.7 fusion
  1.4 0.6 maximum_bitcast_fusion.route_ref.refs_0_
  2.0 3.6 select.5
  5.7 5.3 %all-to-all-start.1 = ((bf16[8,2,40,1792]{3,2,1,0:T(8,128)(2,1)}), bf16[8,2,40,1792]{3,2,1,0:T(8,128)(2,1)}, u32[]{:S(2)}, u32[]{:S(2)}) async-start(bf16[8,2,40,1792]{3,2,1,0:T(8,128)(2,1)} %select.5), calls=%async_computation.1 | async-start | bytes 4587520 | tf_op jit(solution)/shard_map/all_to_all | solution.py:232
  11.0 2.3 collective-permute-start.3
  13.3 0.1 collective-permute-start.2
  13.4 21.0 %collective-permute-done.2.route_ref.refs_0_ = bf16[24,256]{1,0:T(8,128)(2,1)S(1)} collective-permute-done((bf16[24,256]{1,0:T(8,128)(2,1)S(1)}, bf16[24,256]{1,0:T(8,128)(2,1)S(1)}, u32[]{:S(2)}, u32[]{:S(2)}) %collective-permute-start.2) | collective-permute-done | bytes 12320 | tf_op jit(solution)/shard_map/ppermute | solution.py:229
  34.4 0.6 copy-done.6
  35.0 0.0 collective-permute-done.3.x_ref
  35.0 3.7 select.6
  38.6 0.3 all-to-all-done.1.refs_1_
  38.9 4.4 %all-to-all-start.3 = ((bf16[8,2,40,1792]{3,2,1,0:T(8,128)(2,1)}), bf16[8,2,40,1792]{3,2,1,0:T(8,128)(2,1)}, u32[]{:S(2)}, u32[]{:S(2)}) async-start(bf16[8,2,40,1792]{3,2,1,0:T(8,128)(2,1)} %select.6), calls=%async_computation.3 | async-start | bytes 4587520 | tf_op jit(solution)/shard_map/all_to_all | solution.py:232
  43.3 4.2 collective-permute-start.1
  47.6 0.1 collective-permute-start
  47.6 21.1 %collective-permute-done.route_ref.refs_0_ = bf16[24,256]{1,0:T(8,128)(2,1)S(1)} collective-permute-done((bf16[24,256]{1,0:T(8,128)(2,1)S(1)}, bf16[24,256]{1,0:T(8,128)(2,1)S(1)}, u32[]{:S(2)}, u32[]{:S(2)}) %collective-permute-start) | collective-permute-done | bytes 12320 | tf_op jit(solution)/shard_map/ppermute | solution.py:229
  68.7 0.6 copy-done.7
  69.3 0.0 collective-permute-done.1.x_ref
  69.3 3.7 select.4
  73.0 0.0 all-to-all-done.3.refs_0_
  73.0 4.5 %all-to-all-start = ((bf16[8,2,40,1792]{3,2,1,0:T(8,128)(2,1)}), bf16[8,2,40,1792]{3,2,1,0:T(8,128)(2,1)}, u32[]{:S(2)}, u32[]{:S(2)}) async-start(bf16[8,2,40,1792]{3,2,1,0:T(8,128)(2,1)} %select.4), calls=%async_computation | async-start | bytes 4587520 | tf_op jit(solution)/shard_map/all_to_all | solution.py:232
  77.6 20.6 %collective-permute-start.5 = (bf16[256,1792]{1,0:T(8,128)(2,1)S(1)}, bf16[256,1792]{1,0:T(8,128)(2,1)}, u32[]{:S(2)}, u32[]{:S(2)}) collective-permute-start(bf16[256,1792]{1,0:T(8,128)(2,1)S(1)} %bitcast.19), channel_id=1, source_target_pairs={{0,4},{1,5},{2,6},{3,7},{4,0},{5,1},{6,2},{7,3},{8,12},{9,13},{10,... | collective-permute-start | bytes 2752520 | tf_op jit(solution)/shard_map/ppermute | solution.py:229
  98.2 0.1 collective-permute-start.4
  98.3 40.9 %collective-permute-done.4.route_ref.refs_1_ = bf16[24,256]{1,0:T(8,128)(2,1)S(1)} collective-permute-done((bf16[24,256]{1,0:T(8,128)(2,1)S(1)}, bf16[24,256]{1,0:T(8,128)(2,1)S(1)}, u32[]{:S(2)}, u32[]{:S(2)}) %collective-permute-start.4) | collective-permute-done | bytes 12320 | tf_op jit(solution)/shard_map/ppermute | solution.py:229
  139.2 0.6 copy-done.8
  139.8 3.6 select.7
  143.4 0.0 all-to-all-done.refs_0_
  143.4 4.4 %all-to-all-start.4 = ((bf16[8,2,40,1792]{3,2,1,0:T(8,128)(2,1)}), bf16[8,2,40,1792]{3,2,1,0:T(8,128)(2,1)}, u32[]{:S(2)}, u32[]{:S(2)}) async-start(bf16[8,2,40,1792]{3,2,1,0:T(8,128)(2,1)} %select.7), calls=%async_computation.4 | async-start | bytes 4587520 | tf_op jit(solution)/shard_map/all_to_all | solution.py:232
  147.8 44.0 %experts.2 = (bf16[8,2,40,1792]{3,2,1,0:T(8,128)(2,1)}, bf16[8,2,40,1792]{3,2,1,0:T(8,128)(2,1)}) custom-call(bf16[8,2,40,1792]{3,2,1,0:T(8,128)(2,1)} %all-to-all-done.refs_0_, bf16[8,2,40,1792]{3,2,1,0:T(8,128)(2,1)} %all-to-all-done.1.refs_1_, bf16[2,1792,2560]{2,1,0:T(8,128)(2,1)} %refs_2_.3, bf16[2,1792,2560]{2,1,0:T(8,128)(2,1)} %refs_3_.3, ...), custom_call_target="tpu_custom_call" | custom-call | flops 35232153600 | bytes 55050240 | tf_op jit(solution)/shard_map/experts/pallas_call | solution.py:199
  191.9 4.6 %all-to-all-start.6 = ((bf16[8,2,40,1792]{3,2,1,0:T(8,128)(2,1)}), bf16[8,2,40,1792]{3,2,1,0:T(8,128)(2,1)}, u32[]{:S(2)}, u32[]{:S(2)}) async-start(bf16[8,2,40,1792]{3,2,1,0:T(8,128)(2,1)} %get-tuple-element.12), calls=%async_computation.6 | async-start | bytes 4587520 | tf_op jit(solution)/shard_map/all_to_all | solution.py:232
  196.4 44.0 %experts.3 = bf16[8,2,80,1792]{3,2,1,0:T(8,128)(2,1)} custom-call(bf16[8,2,40,1792]{3,2,1,0:T(8,128)(2,1)} %all-to-all-done.3.refs_0_, bf16[8,2,40,1792]{3,2,1,0:T(8,128)(2,1)} %all-to-all-done.4.refs_1_, bf16[2,1792,2560]{2,1,0:T(8,128)(2,1)} %refs_2_.3, bf16[2,1792,2560]{2,1,0:T(8,128)(2,1)} %refs_3_.3, bf16[2,2560,1792]{2,1,0:T(8,128)(2,1)} %refs_4_.3), custom_call_target="tpu_custom_call" | custom-call | flops 35232153600 | bytes 55050240 | tf_op jit(solution)/shard_map/experts/pallas_call | solution.py:199
  240.4 0.0 all-to-all-done.6.v_ref
  240.5 4.6 %all-to-all-start.5 = ((bf16[8,2,80,1792]{3,2,1,0:T(8,128)(2,1)}), bf16[8,2,80,1792]{3,2,1,0:T(8,128)(2,1)}, u32[]{:S(2)}, u32[]{:S(2)}) async-start(bf16[8,2,80,1792]{3,2,1,0:T(8,128)(2,1)} %experts.3), calls=%async_computation.5 | async-start | bytes 9175040 | tf_op jit(solution)/shard_map/all_to_all | solution.py:232
  245.1 25.9 %shared.5.refs_0_ = f32[256,1792]{1,0:T(8,128)} custom-call(bf16[256,1792]{1,0:T(8,128)(2,1)} %bitcast.12, bf16[1792,20480]{1,0:T(8,128)(2,1)} %g_ref.9, bf16[1792,20480]{1,0:T(8,128)(2,1)} %u_ref.9, bf16[20480,1792]{1,0:T(8,128)(2,1)} %d_ref.9), custom_call_target="tpu_custom_call" | custom-call | flops 14092861440 | bytes 55050240 | tf_op jit(solution)/shard_map/shared/pallas_call | solution.py:137
  271.0 22.4 %shared.6.refs_0_ = f32[256,1792]{1,0:T(8,128)} custom-call(bf16[256,1792]{1,0:T(8,128)(2,1)} %bitcast.13, bf16[1792,20480]{1,0:T(8,128)(2,1)} %g_ref.9, bf16[1792,20480]{1,0:T(8,128)(2,1)} %u_ref.9, bf16[20480,1792]{1,0:T(8,128)(2,1)} %d_ref.9, f32[256,1792]{1,0:T(8,128)} %shared.5.refs_0_), custom_call_target="tpu_custom_call" | custom-call | flops 11274289152 | bytes 44040192 | tf_op jit(solution)/shard_map/shared/pallas_call | solution.py:137
  293.4 22.2 %shared.7.refs_0_ = f32[256,1792]{1,0:T(8,128)} custom-call(bf16[256,1792]{1,0:T(8,128)(2,1)} %bitcast.14, bf16[1792,20480]{1,0:T(8,128)(2,1)} %g_ref.9, bf16[1792,20480]{1,0:T(8,128)(2,1)} %u_ref.9, bf16[20480,1792]{1,0:T(8,128)(2,1)} %d_ref.9, f32[256,1792]{1,0:T(8,128)} %shared.6.refs_0_), custom_call_target="tpu_custom_call" | custom-call | flops 11274289152 | bytes 44040192 | tf_op jit(solution)/shard_map/shared/pallas_call | solution.py:137
  315.6 4.6 %all-to-all-start.2 = ((bf16[8,2,40,1792]{3,2,1,0:T(8,128)(2,1)}), bf16[8,2,40,1792]{3,2,1,0:T(8,128)(2,1)}, u32[]{:S(2)}, u32[]{:S(2)}) async-start(bf16[8,2,40,1792]{3,2,1,0:T(8,128)(2,1)} %get-tuple-element.9), calls=%async_computation.2 | async-start | bytes 4587520 | tf_op jit(solution)/shard_map/all_to_all | solution.py:232
  320.2 18.7 %shared.8.refs_0_ = f32[256,1792]{1,0:T(8,128)} custom-call(bf16[256,1792]{1,0:T(8,128)(2,1)} %bitcast.15, bf16[1792,20480]{1,0:T(8,128)(2,1)} %g_ref.9, bf16[1792,20480]{1,0:T(8,128)(2,1)} %u_ref.9, bf16[20480,1792]{1,0:T(8,128)(2,1)} %d_ref.9, f32[256,1792]{1,0:T(8,128)} %shared.7.refs_0_), custom_call_target="tpu_custom_call" | custom-call | flops 8455716864 | bytes 33030144 | tf_op jit(solution)/shard_map/shared/pallas_call | solution.py:137
  338.9 3.6 combine.4
  342.5 1.3 collective-permute-start.8
  343.9 5.3 %combine.3 = (bf16[256,1792]{1,0:T(8,128)(2,1)}, bf16[256,1792]{1,0:T(8,128)(2,1)}) custom-call(s32[1]{0:T(128)} %bitcast.z_ref, bf16[8,2,80,1792]{3,2,1,0:T(8,128)(2,1)} %all-to-all-done.5.v_ref, bf16[24,256]{1,0:T(8,128)(2,1)} %copy-done.6, bf16[24,256]{1,0:T(8,128)(2,1)} %copy-done.8), custom_call_target="tpu_custom_call" | custom-call | flops 1174405120 | bytes 4587520 | tf_op jit(solution)/shard_map/combine/pallas_call | solution.py:102
  349.2 3.0 collective-permute-start.7
  352.2 22.2 %shared.9.refs_1_ = f32[256,1792]{1,0:T(8,128)} custom-call(bf16[256,1792]{1,0:T(8,128)(2,1)} %bitcast.16, bf16[1792,20480]{1,0:T(8,128)(2,1)} %g_ref.9, bf16[1792,20480]{1,0:T(8,128)(2,1)} %u_ref.9, bf16[20480,1792]{1,0:T(8,128)(2,1)} %d_ref.9, f32[256,1792]{1,0:T(8,128)} %shared.8.refs_0_), custom_call_target="tpu_custom_call" | custom-call | flops 11274289152 | bytes 44040192 | tf_op jit(solution)/shard_map/shared/pallas_call | solution.py:137
  374.5 0.0 all-to-all-done.2.v_ref
  374.5 0.0 collective-permute-done.8.refs_4_
  374.5 16.5 %collective-permute-done.6.refs_2_ = bf16[256,1792]{1,0:T(8,128)(2,1)} collective-permute-done((bf16[256,1792]{1,0:T(8,128)(2,1)}, bf16[256,1792]{1,0:T(8,128)(2,1)}, u32[]{:S(2)}, u32[]{:S(2)}) %collective-permute-start.6) | collective-permute-done | bytes 917536 | tf_op jit(solution)/shard_map/ppermute | solution.py:229
  391.0 31.5 %collective-permute-done.7.refs_3_ = bf16[256,1792]{1,0:T(8,128)(2,1)} collective-permute-done((bf16[256,1792]{1,0:T(8,128)(2,1)}, bf16[256,1792]{1,0:T(8,128)(2,1)}, u32[]{:S(2)}, u32[]{:S(2)}) %collective-permute-start.7) | collective-permute-done | bytes 917536 | tf_op jit(solution)/shard_map/ppermute | solution.py:229
  422.4 4.6 %combine.5 = bf16[256,1792]{1,0:T(8,128)(2,1)} custom-call(s32[1]{0:T(128)} %bitcast.z_ref, bf16[8,2,40,1792]{3,2,1,0:T(8,128)(2,1)} %all-to-all-done.2.v_ref, bf16[24,256]{1,0:T(8,128)(2,1)} %maximum_bitcast_fusion.route_ref.refs_0_, f32[256,1792]{1,0:T(8,128)} %shared.9.refs_1_, bf16[256,1792]{1,0:T(8,128)(2,1)} %collective-permute-done.6.refs_2_, ...), custom_call_target="tpu_custom_call" | custom-call | flops 587202560 | bytes 2293760 | tf_op jit(solution)/shard_map/combine/pallas_call | solution.py:102
  (19 shorter events, 0.0 us)
Async XLA Ops:
  5.7 5.3 %copy-start = (bf16[1,1,256,1792]{3,2,1,0:T(8,128)(2,1)S(1)}, bf16[1,1,256,1792]{3,2,1,0:T(8,128)(2,1)}, u32[]{:S(2)}) copy-start(bf16[1,1,256,1792]{3,2,1,0:T(8,128)(2,1)} %param.10) | copy-start | bytes 2752516
  5.7 7.6 %copy-start.3 = (bf16[24,256]{1,0:T(8,128)(2,1)S(1)}, bf16[24,256]{1,0:T(8,128)(2,1)}, u32[]{:S(2)}) copy-start(bf16[24,256]{1,0:T(8,128)(2,1)} %maximum_bitcast_fusion.route_ref.refs_0_) | copy-start | bytes 36868
  5.7 33.3 %all-to-all-start.1 = ((bf16[8,2,40,1792]{3,2,1,0:T(8,128)(2,1)}), bf16[8,2,40,1792]{3,2,1,0:T(8,128)(2,1)}, u32[]{:S(2)}, u32[]{:S(2)}) async-start(bf16[8,2,40,1792]{3,2,1,0:T(8,128)(2,1)} %select.5), calls=%async_computation.1 | async-start | bytes 4587520 | tf_op jit(solution)/shard_map/all_to_all | solution.py:232
  11.0 24.0 %collective-permute-start.3 = (bf16[256,1792]{1,0:T(8,128)(2,1)S(1)}, bf16[256,1792]{1,0:T(8,128)(2,1)}, u32[]{:S(2)}, u32[]{:S(2)}) collective-permute-start(bf16[256,1792]{1,0:T(8,128)(2,1)S(1)} %bitcast.17), channel_id=1, source_target_pairs={{0,2},{1,3},{2,0},{3,1},{4,6},{5,7},{6,4},{7,5},{8,10},{9,11},{10,... | collective-permute-start | bytes 2752520 | tf_op jit(solution)/shard_map/ppermute | solution.py:229
  13.3 21.1 %collective-permute-start.2 = (bf16[24,256]{1,0:T(8,128)(2,1)S(1)}, bf16[24,256]{1,0:T(8,128)(2,1)S(1)}, u32[]{:S(2)}, u32[]{:S(2)}) collective-permute-start(bf16[24,256]{1,0:T(8,128)(2,1)S(1)} %copy-done.3), channel_id=1, source_target_pairs={{0,2},{1,3},{2,0},{3,1},{4,6},{5,7},{6,4},{7,5},{8,10},{9,11},{10,... | collective-permute-start | bytes 36872 | tf_op jit(solution)/shard_map/ppermute | solution.py:229
  34.4 0.6 copy-start.6
  38.6 4.7 %copy-start.1 = (bf16[1,1,256,1792]{3,2,1,0:T(8,128)(2,1)S(1)}, bf16[1,1,256,1792]{3,2,1,0:T(8,128)(2,1)}, u32[]{:S(2)}) copy-start(bf16[1,1,256,1792]{3,2,1,0:T(8,128)(2,1)} %param.10) | copy-start | bytes 2752516
  38.6 8.9 %copy-start.4 = (bf16[24,256]{1,0:T(8,128)(2,1)S(1)}, bf16[24,256]{1,0:T(8,128)(2,1)}, u32[]{:S(2)}) copy-start(bf16[24,256]{1,0:T(8,128)(2,1)} %maximum_bitcast_fusion.route_ref.refs_0_) | copy-start | bytes 36868
  38.9 34.1 %all-to-all-start.3 = ((bf16[8,2,40,1792]{3,2,1,0:T(8,128)(2,1)}), bf16[8,2,40,1792]{3,2,1,0:T(8,128)(2,1)}, u32[]{:S(2)}, u32[]{:S(2)}) async-start(bf16[8,2,40,1792]{3,2,1,0:T(8,128)(2,1)} %select.6), calls=%async_computation.3 | async-start | bytes 4587520 | tf_op jit(solution)/shard_map/all_to_all | solution.py:232
  43.3 26.0 %collective-permute-start.1 = (bf16[256,1792]{1,0:T(8,128)(2,1)S(1)}, bf16[256,1792]{1,0:T(8,128)(2,1)}, u32[]{:S(2)}, u32[]{:S(2)}) collective-permute-start(bf16[256,1792]{1,0:T(8,128)(2,1)S(1)} %bitcast.18), channel_id=1, source_target_pairs={{0,6},{1,7},{2,4},{3,5},{4,2},{5,3},{6,0},{7,1},{8,14},{9,15},{10,... | collective-permute-start | bytes 2752520 | tf_op jit(solution)/shard_map/ppermute | solution.py:229
  47.6 21.2 %collective-permute-start = (bf16[24,256]{1,0:T(8,128)(2,1)S(1)}, bf16[24,256]{1,0:T(8,128)(2,1)S(1)}, u32[]{:S(2)}, u32[]{:S(2)}) collective-permute-start(bf16[24,256]{1,0:T(8,128)(2,1)S(1)} %copy-done.4), channel_id=1, source_target_pairs={{0,6},{1,7},{2,4},{3,5},{4,2},{5,3},{6,0},{7,1},{8,14},{9,15},{10,... | collective-permute-start | bytes 36872 | tf_op jit(solution)/shard_map/ppermute | solution.py:229
  68.7 0.6 copy-start.7
  73.0 4.5 %copy-start.2 = (bf16[1,1,256,1792]{3,2,1,0:T(8,128)(2,1)S(1)}, bf16[1,1,256,1792]{3,2,1,0:T(8,128)(2,1)}, u32[]{:S(2)}) copy-start(bf16[1,1,256,1792]{3,2,1,0:T(8,128)(2,1)} %param.10) | copy-start | bytes 2752516
  73.0 25.2 %copy-start.5 = (bf16[24,256]{1,0:T(8,128)(2,1)S(1)}, bf16[24,256]{1,0:T(8,128)(2,1)}, u32[]{:S(2)}) copy-start(bf16[24,256]{1,0:T(8,128)(2,1)} %maximum_bitcast_fusion.route_ref.refs_0_) | copy-start | bytes 36868
  73.0 70.4 %all-to-all-start = ((bf16[8,2,40,1792]{3,2,1,0:T(8,128)(2,1)}), bf16[8,2,40,1792]{3,2,1,0:T(8,128)(2,1)}, u32[]{:S(2)}, u32[]{:S(2)}) async-start(bf16[8,2,40,1792]{3,2,1,0:T(8,128)(2,1)} %select.4), calls=%async_computation | async-start | bytes 4587520 | tf_op jit(solution)/shard_map/all_to_all | solution.py:232
  77.6 62.2 %collective-permute-start.5 = (bf16[256,1792]{1,0:T(8,128)(2,1)S(1)}, bf16[256,1792]{1,0:T(8,128)(2,1)}, u32[]{:S(2)}, u32[]{:S(2)}) collective-permute-start(bf16[256,1792]{1,0:T(8,128)(2,1)S(1)} %bitcast.19), channel_id=1, source_target_pairs={{0,4},{1,5},{2,6},{3,7},{4,0},{5,1},{6,2},{7,3},{8,12},{9,13},{10,... | collective-permute-start | bytes 2752520 | tf_op jit(solution)/shard_map/ppermute | solution.py:229
  98.2 41.0 %collective-permute-start.4 = (bf16[24,256]{1,0:T(8,128)(2,1)S(1)}, bf16[24,256]{1,0:T(8,128)(2,1)S(1)}, u32[]{:S(2)}, u32[]{:S(2)}) collective-permute-start(bf16[24,256]{1,0:T(8,128)(2,1)S(1)} %copy-done.5), channel_id=1, source_target_pairs={{0,4},{1,5},{2,6},{3,7},{4,0},{5,1},{6,2},{7,3},{8,12},{9,13},{10,... | collective-permute-start | bytes 36872 | tf_op jit(solution)/shard_map/ppermute | solution.py:229
  139.2 0.6 copy-start.8
  143.4 48.4 %all-to-all-start.4 = ((bf16[8,2,40,1792]{3,2,1,0:T(8,128)(2,1)}), bf16[8,2,40,1792]{3,2,1,0:T(8,128)(2,1)}, u32[]{:S(2)}, u32[]{:S(2)}) async-start(bf16[8,2,40,1792]{3,2,1,0:T(8,128)(2,1)} %select.7), calls=%async_computation.4 | async-start | bytes 4587520 | tf_op jit(solution)/shard_map/all_to_all | solution.py:232
  191.9 48.6 %all-to-all-start.6 = ((bf16[8,2,40,1792]{3,2,1,0:T(8,128)(2,1)}), bf16[8,2,40,1792]{3,2,1,0:T(8,128)(2,1)}, u32[]{:S(2)}, u32[]{:S(2)}) async-start(bf16[8,2,40,1792]{3,2,1,0:T(8,128)(2,1)} %get-tuple-element.12), calls=%async_computation.6 | async-start | bytes 4587520 | tf_op jit(solution)/shard_map/all_to_all | solution.py:232
  240.5 75.1 %all-to-all-start.5 = ((bf16[8,2,80,1792]{3,2,1,0:T(8,128)(2,1)}), bf16[8,2,80,1792]{3,2,1,0:T(8,128)(2,1)}, u32[]{:S(2)}, u32[]{:S(2)}) async-start(bf16[8,2,80,1792]{3,2,1,0:T(8,128)(2,1)} %experts.3), calls=%async_computation.5 | async-start | bytes 9175040 | tf_op jit(solution)/shard_map/all_to_all | solution.py:232
  315.6 58.9 %all-to-all-start.2 = ((bf16[8,2,40,1792]{3,2,1,0:T(8,128)(2,1)}), bf16[8,2,40,1792]{3,2,1,0:T(8,128)(2,1)}, u32[]{:S(2)}, u32[]{:S(2)}) async-start(bf16[8,2,40,1792]{3,2,1,0:T(8,128)(2,1)} %get-tuple-element.9), calls=%async_computation.2 | async-start | bytes 4587520 | tf_op jit(solution)/shard_map/all_to_all | solution.py:232
  342.5 31.9 %collective-permute-start.8 = (bf16[256,1792]{1,0:T(8,128)(2,1)}, bf16[256,1792]{1,0:T(8,128)(2,1)}, u32[]{:S(2)}, u32[]{:S(2)}) collective-permute-start(bf16[256,1792]{1,0:T(8,128)(2,1)} %combine.4), channel_id=1, source_target_pairs={{0,6},{1,7},{2,4},{3,5},{4,2},{5,3},{6,0},{7,1},{8,14},{9,15},{10,... | collective-permute-start | bytes 2752520 | tf_op jit(solution)/shard_map/ppermute | solution.py:229
  349.2 41.8 %collective-permute-start.6 = (bf16[256,1792]{1,0:T(8,128)(2,1)}, bf16[256,1792]{1,0:T(8,128)(2,1)}, u32[]{:S(2)}, u32[]{:S(2)}) collective-permute-start(bf16[256,1792]{1,0:T(8,128)(2,1)} %get-tuple-element.10), channel_id=1, source_target_pairs={{0,2},{1,3},{2,0},{3,1},{4,6},{5,7},{6,4},{7,5},{8,10},{9,11},{10,... | collective-permute-start | bytes 2752520 | tf_op jit(solution)/shard_map/ppermute | solution.py:229
  349.2 73.2 %collective-permute-start.7 = (bf16[256,1792]{1,0:T(8,128)(2,1)}, bf16[256,1792]{1,0:T(8,128)(2,1)}, u32[]{:S(2)}, u32[]{:S(2)}) collective-permute-start(bf16[256,1792]{1,0:T(8,128)(2,1)} %get-tuple-element.11), channel_id=1, source_target_pairs={{0,4},{1,5},{2,6},{3,7},{4,0},{5,1},{6,2},{7,3},{8,12},{9,13},{10,... | collective-permute-start | bytes 2752520 | tf_op jit(solution)/shard_map/ppermute | solution.py:229

commit v3 on v2

--- a/solution.py
+++ b/solution.py
@@ -260,9 +260,12 @@
         arrived = []
         for i, group in enumerate(BACK):
             v = exchange(outs[i])
-            parts = combine(z, v, [routes[k] for k in group], () if any(group) else (shared, *arrived))
+            adds = (shared, *arrived) if group == (0,) else (relayed,) if group == (3,) else ()
+            parts = combine(z, v, [routes[k] for k in group], adds)
             for k, part in zip(group, parts):
-                if k:
+                if k == 2:
+                    relayed = shift(part, 1)
+                elif k:
                     arrived.append(shift(part, k))
         return parts[0][None, None]
 

time: 428 us -> 404 us (0.944)
  waiting for transfers between devices: 131 us -> 107 us
    ppermute x9, waiting for transfers between devices: 131 us -> 98.1 us  [shift(): return lax.ppermute(v, 'ep', [(i, i ^ 2 * k) for i in range(n)])]
    all_to_all x7, waiting for transfers between devices: 0.31 us -> 8.57 us  [exchange(): return lax.all_to_all(v, 'ep', 0, 0, axis_index_groups=planes, tiled=True)]
  transfers between devices with their start and end apart: 16 -> 16, of which waited for: 6 -> 6; matrix products, arithmetic and copies ran while one was open for 0% -> 0% of each run, Pallas kernels for 51% -> 55%
where the time goes in v3:
time: 404 us; the launch traced here: 400 us
  Pallas kernels  228 us (56%)
  waiting for transfers between devices  107 us (26%)
  starting transfers between devices  61.8 us (15%)
    pallas_call x5, Pallas kernels, shared_part(): pl.pallas_call(functools.partial(shared_kernel, total is not None), grid=...  111 us
    ppermute x9, waiting for transfers between devices, shift(): return lax.ppermute(v, 'ep', [(i, i ^ 2 * k) for i in range(n)])  98.1 us
    pallas_call x2, Pallas kernels, experts_of(): pl.pallas_call(functools.partial(expert_kernel, len(vs)), grid=(mine, ff...  88 us
    all_to_all x7, starting transfers between devices, exchange(): return lax.all_to_all(v, 'ep', 0, 0, axis_index_groups=planes, tiled=True)  32.3 us
    ppermute x9, starting transfers between devices, shift(): return lax.ppermute(v, 'ep', [(i, i ^ 2 * k) for i in range(n)])  29.5 us
    pallas_call x4, Pallas kernels, select(): pl.pallas_call(select_kernel, grid_spec=pltpu.PrefetchScalarGridSpec(num_...  14.6 us
    pallas_call x3, Pallas kernels, combine(): pl.pallas_call(functools.partial(combine_kernel, parts, len(adds)), grid_...  13.6 us
    all_to_all x7, waiting for transfers between devices, exchange(): return lax.all_to_all(v, 'ep', 0, 0, axis_index_groups=planes, tiled=True)  8.57 us
  transfers between devices with their start and end apart: 16, of which 6 were waited for; matrix products, arithmetic and copies ran while one was open for 0% of the time, Pallas kernels for 55%

profile of v3, /device:TPU:0, one launch (start us, length us, event | category | flops | bytes accessed | tf_op | source)
XLA Modules:
  0.0 400.1 jit_solution(1762335984917954032)
XLA Ops:
  0.0 0.7 convert_bitcast_fusion
  0.7 0.7 fusion
  1.4 0.6 maximum_bitcast_fusion.route_ref.refs_0_
  2.0 3.6 select.5
  5.7 5.3 %all-to-all-start.1 = ((bf16[8,2,40,1792]{3,2,1,0:T(8,128)(2,1)}), bf16[8,2,40,1792]{3,2,1,0:T(8,128)(2,1)}, u32[]{:S(2)}, u32[]{:S(2)}) async-start(bf16[8,2,40,1792]{3,2,1,0:T(8,128)(2,1)} %select.5), calls=%async_computation.1 | async-start | bytes 4587520 | tf_op jit(solution)/shard_map/all_to_all | solution.py:232
  11.0 2.3 collective-permute-start.3
  13.3 0.1 collective-permute-start.2
  13.4 21.0 %collective-permute-done.2.route_ref.refs_0_ = bf16[24,256]{1,0:T(8,128)(2,1)S(1)} collective-permute-done((bf16[24,256]{1,0:T(8,128)(2,1)S(1)}, bf16[24,256]{1,0:T(8,128)(2,1)S(1)}, u32[]{:S(2)}, u32[]{:S(2)}) %collective-permute-start.2) | collective-permute-done | bytes 12320 | tf_op jit(solution)/shard_map/ppermute | solution.py:229
  34.4 0.6 copy-done.6
  35.0 0.0 collective-permute-done.3.x_ref
  35.0 3.6 select.6
  38.6 0.3 all-to-all-done.1.refs_1_
  38.9 4.4 %all-to-all-start.3 = ((bf16[8,2,40,1792]{3,2,1,0:T(8,128)(2,1)}), bf16[8,2,40,1792]{3,2,1,0:T(8,128)(2,1)}, u32[]{:S(2)}, u32[]{:S(2)}) async-start(bf16[8,2,40,1792]{3,2,1,0:T(8,128)(2,1)} %select.6), calls=%async_computation.3 | async-start | bytes 4587520 | tf_op jit(solution)/shard_map/all_to_all | solution.py:232
  43.3 3.2 collective-permute-start.5
  46.5 0.1 collective-permute-start.4
  46.6 40.9 %collective-permute-done.4.route_ref.refs_1_ = bf16[24,256]{1,0:T(8,128)(2,1)S(1)} collective-permute-done((bf16[24,256]{1,0:T(8,128)(2,1)S(1)}, bf16[24,256]{1,0:T(8,128)(2,1)S(1)}, u32[]{:S(2)}, u32[]{:S(2)}) %collective-permute-start.4) | collective-permute-done | bytes 12320 | tf_op jit(solution)/shard_map/ppermute | solution.py:229
  87.5 0.6 copy-done.8
  88.1 3.6 select.7
  91.8 4.5 %all-to-all-start.4 = ((bf16[8,2,40,1792]{3,2,1,0:T(8,128)(2,1)}), bf16[8,2,40,1792]{3,2,1,0:T(8,128)(2,1)}, u32[]{:S(2)}, u32[]{:S(2)}) async-start(bf16[8,2,40,1792]{3,2,1,0:T(8,128)(2,1)} %select.7), calls=%async_computation.4 | async-start | bytes 4587520 | tf_op jit(solution)/shard_map/all_to_all | solution.py:232
  96.3 3.6 collective-permute-start.1
  99.9 0.3 collective-permute-start
  100.2 20.9 %collective-permute-done.route_ref.refs_0_ = bf16[24,256]{1,0:T(8,128)(2,1)S(1)} collective-permute-done((bf16[24,256]{1,0:T(8,128)(2,1)S(1)}, bf16[24,256]{1,0:T(8,128)(2,1)S(1)}, u32[]{:S(2)}, u32[]{:S(2)}) %collective-permute-start) | collective-permute-done | bytes 12320 | tf_op jit(solution)/shard_map/ppermute | solution.py:229
  121.1 0.6 copy-done.7
  121.7 3.6 select.4
  125.3 0.0 all-to-all-done.4.refs_1_
  125.3 4.4 %all-to-all-start = ((bf16[8,2,40,1792]{3,2,1,0:T(8,128)(2,1)}), bf16[8,2,40,1792]{3,2,1,0:T(8,128)(2,1)}, u32[]{:S(2)}, u32[]{:S(2)}) async-start(bf16[8,2,40,1792]{3,2,1,0:T(8,128)(2,1)} %select.4), calls=%async_computation | async-start | bytes 4587520 | tf_op jit(solution)/shard_map/all_to_all | solution.py:232
  129.7 44.0 %experts.3 = bf16[8,2,80,1792]{3,2,1,0:T(8,128)(2,1)} custom-call(bf16[8,2,40,1792]{3,2,1,0:T(8,128)(2,1)} %all-to-all-done.3.refs_0_, bf16[8,2,40,1792]{3,2,1,0:T(8,128)(2,1)} %all-to-all-done.4.refs_1_, bf16[2,1792,2560]{2,1,0:T(8,128)(2,1)} %refs_2_.3, bf16[2,1792,2560]{2,1,0:T(8,128)(2,1)} %refs_3_.3, bf16[2,2560,1792]{2,1,0:T(8,128)(2,1)} %refs_4_.3), custom_call_target="tpu_custom_call" | custom-call | flops 35232153600 | bytes 55050240 | tf_op jit(solution)/shard_map/experts/pallas_call | solution.py:199
  173.7 0.0 all-to-all-done.refs_0_
  173.7 4.8 %all-to-all-start.5 = ((bf16[8,2,80,1792]{3,2,1,0:T(8,128)(2,1)}), bf16[8,2,80,1792]{3,2,1,0:T(8,128)(2,1)}, u32[]{:S(2)}, u32[]{:S(2)}) async-start(bf16[8,2,80,1792]{3,2,1,0:T(8,128)(2,1)} %experts.3), calls=%async_computation.5 | async-start | bytes 9175040 | tf_op jit(solution)/shard_map/all_to_all | solution.py:232
  178.5 44.0 %experts.2 = (bf16[8,2,40,1792]{3,2,1,0:T(8,128)(2,1)}, bf16[8,2,40,1792]{3,2,1,0:T(8,128)(2,1)}) custom-call(bf16[8,2,40,1792]{3,2,1,0:T(8,128)(2,1)} %all-to-all-done.refs_0_, bf16[8,2,40,1792]{3,2,1,0:T(8,128)(2,1)} %all-to-all-done.1.refs_1_, bf16[2,1792,2560]{2,1,0:T(8,128)(2,1)} %refs_2_.3, bf16[2,1792,2560]{2,1,0:T(8,128)(2,1)} %refs_3_.3, ...), custom_call_target="tpu_custom_call" | custom-call | flops 35232153600 | bytes 55050240 | tf_op jit(solution)/shard_map/experts/pallas_call | solution.py:199
  222.5 8.3 %all-to-all-done.5.v_ref = bf16[8,2,80,1792]{3,2,1,0:T(8,128)(2,1)} async-done(((bf16[8,2,80,1792]{3,2,1,0:T(8,128)(2,1)}), bf16[8,2,80,1792]{3,2,1,0:T(8,128)(2,1)}, u32[]{:S(2)}, u32[]{:S(2)}) %all-to-all-start.5) | async-done | bytes 4587552 | tf_op jit(solution)/shard_map/all_to_all | solution.py:232
  230.8 4.4 %all-to-all-start.6 = ((bf16[8,2,40,1792]{3,2,1,0:T(8,128)(2,1)}), bf16[8,2,40,1792]{3,2,1,0:T(8,128)(2,1)}, u32[]{:S(2)}, u32[]{:S(2)}) async-start(bf16[8,2,40,1792]{3,2,1,0:T(8,128)(2,1)} %get-tuple-element.11), calls=%async_computation.6 | async-start | bytes 4587520 | tf_op jit(solution)/shard_map/all_to_all | solution.py:232
  235.1 25.9 %shared.5.refs_0_ = f32[256,1792]{1,0:T(8,128)} custom-call(bf16[256,1792]{1,0:T(8,128)(2,1)} %bitcast.12, bf16[1792,20480]{1,0:T(8,128)(2,1)} %g_ref.9, bf16[1792,20480]{1,0:T(8,128)(2,1)} %u_ref.9, bf16[20480,1792]{1,0:T(8,128)(2,1)} %d_ref.9), custom_call_target="tpu_custom_call" | custom-call | flops 14092861440 | bytes 55050240 | tf_op jit(solution)/shard_map/shared/pallas_call | solution.py:137
  261.1 22.6 %shared.6.refs_0_ = f32[256,1792]{1,0:T(8,128)} custom-call(bf16[256,1792]{1,0:T(8,128)(2,1)} %bitcast.13, bf16[1792,20480]{1,0:T(8,128)(2,1)} %g_ref.9, bf16[1792,20480]{1,0:T(8,128)(2,1)} %u_ref.9, bf16[20480,1792]{1,0:T(8,128)(2,1)} %d_ref.9, f32[256,1792]{1,0:T(8,128)} %shared.5.refs_0_), custom_call_target="tpu_custom_call" | custom-call | flops 11274289152 | bytes 44040192 | tf_op jit(solution)/shard_map/shared/pallas_call | solution.py:137
  283.7 5.3 %combine.3 = (bf16[256,1792]{1,0:T(8,128)(2,1)}, bf16[256,1792]{1,0:T(8,128)(2,1)}) custom-call(s32[1]{0:T(128)} %bitcast.z_ref, bf16[8,2,80,1792]{3,2,1,0:T(8,128)(2,1)} %all-to-all-done.5.v_ref, bf16[24,256]{1,0:T(8,128)(2,1)} %copy-done.6, bf16[24,256]{1,0:T(8,128)(2,1)} %copy-done.8), custom_call_target="tpu_custom_call" | custom-call | flops 1174405120 | bytes 4587520 | tf_op jit(solution)/shard_map/combine/pallas_call | solution.py:102
  289.0 18.8 %collective-permute-start.7 = (bf16[256,1792]{1,0:T(8,128)(2,1)}, bf16[256,1792]{1,0:T(8,128)(2,1)}, u32[]{:S(2)}, u32[]{:S(2)}) collective-permute-start(bf16[256,1792]{1,0:T(8,128)(2,1)} %get-tuple-element.12), channel_id=1, source_target_pairs={{0,2},{1,3},{2,0},{3,1},{4,6},{5,7},{6,4},{7,5},{8,10},{9,11},{10,... | collective-permute-start | bytes 2752520 | tf_op jit(solution)/shard_map/ppermute | solution.py:229
  307.8 0.0 all-to-all-done.6.v_ref
  307.8 4.6 %all-to-all-start.2 = ((bf16[8,2,40,1792]{3,2,1,0:T(8,128)(2,1)}), bf16[8,2,40,1792]{3,2,1,0:T(8,128)(2,1)}, u32[]{:S(2)}, u32[]{:S(2)}) async-start(bf16[8,2,40,1792]{3,2,1,0:T(8,128)(2,1)} %get-tuple-element.9), calls=%async_computation.2 | async-start | bytes 4587520 | tf_op jit(solution)/shard_map/all_to_all | solution.py:232
  312.4 22.1 %shared.7.refs_0_ = f32[256,1792]{1,0:T(8,128)} custom-call(bf16[256,1792]{1,0:T(8,128)(2,1)} %bitcast.14, bf16[1792,20480]{1,0:T(8,128)(2,1)} %g_ref.9, bf16[1792,20480]{1,0:T(8,128)(2,1)} %u_ref.9, bf16[20480,1792]{1,0:T(8,128)(2,1)} %d_ref.9, f32[256,1792]{1,0:T(8,128)} %shared.6.refs_0_), custom_call_target="tpu_custom_call" | custom-call | flops 11274289152 | bytes 44040192 | tf_op jit(solution)/shard_map/shared/pallas_call | solution.py:137
  334.5 18.7 %shared.8.refs_0_ = f32[256,1792]{1,0:T(8,128)} custom-call(bf16[256,1792]{1,0:T(8,128)(2,1)} %bitcast.15, bf16[1792,20480]{1,0:T(8,128)(2,1)} %g_ref.9, bf16[1792,20480]{1,0:T(8,128)(2,1)} %u_ref.9, bf16[20480,1792]{1,0:T(8,128)(2,1)} %d_ref.9, f32[256,1792]{1,0:T(8,128)} %shared.7.refs_0_), custom_call_target="tpu_custom_call" | custom-call | flops 8455716864 | bytes 33030144 | tf_op jit(solution)/shard_map/shared/pallas_call | solution.py:137
  353.2 0.0 collective-permute-start.6
  353.2 0.0 collective-permute-done.7.refs_1_
  353.2 3.8 combine.4
  357.0 1.2 collective-permute-start.8
  358.2 22.1 %shared.9.refs_1_ = f32[256,1792]{1,0:T(8,128)} custom-call(bf16[256,1792]{1,0:T(8,128)(2,1)} %bitcast.16, bf16[1792,20480]{1,0:T(8,128)(2,1)} %g_ref.9, bf16[1792,20480]{1,0:T(8,128)(2,1)} %u_ref.9, bf16[20480,1792]{1,0:T(8,128)(2,1)} %d_ref.9, f32[256,1792]{1,0:T(8,128)} %shared.8.refs_0_), custom_call_target="tpu_custom_call" | custom-call | flops 11274289152 | bytes 44040192 | tf_op jit(solution)/shard_map/shared/pallas_call | solution.py:137
  380.3 15.3 %collective-permute-done.6.refs_2_ = bf16[256,1792]{1,0:T(8,128)(2,1)} collective-permute-done((bf16[256,1792]{1,0:T(8,128)(2,1)}, bf16[256,1792]{1,0:T(8,128)(2,1)}, u32[]{:S(2)}, u32[]{:S(2)}) %collective-permute-start.6) | collective-permute-done | bytes 917536 | tf_op jit(solution)/shard_map/ppermute | solution.py:229
  395.6 0.0 collective-permute-done.8.refs_3_
  395.6 4.5 %combine.5 = bf16[256,1792]{1,0:T(8,128)(2,1)} custom-call(s32[1]{0:T(128)} %bitcast.z_ref, bf16[8,2,40,1792]{3,2,1,0:T(8,128)(2,1)} %all-to-all-done.2.v_ref, bf16[24,256]{1,0:T(8,128)(2,1)} %maximum_bitcast_fusion.route_ref.refs_0_, f32[256,1792]{1,0:T(8,128)} %shared.9.refs_1_, bf16[256,1792]{1,0:T(8,128)(2,1)} %collective-permute-done.6.refs_2_, ...), custom_call_target="tpu_custom_call" | custom-call | flops 587202560 | bytes 2293760 | tf_op jit(solution)/shard_map/combine/pallas_call | solution.py:102
  (19 shorter events, 0.0 us)
Async XLA Ops:
  5.7 5.3 %copy-start = (bf16[1,1,256,1792]{3,2,1,0:T(8,128)(2,1)S(1)}, bf16[1,1,256,1792]{3,2,1,0:T(8,128)(2,1)}, u32[]{:S(2)}) copy-start(bf16[1,1,256,1792]{3,2,1,0:T(8,128)(2,1)} %param.10) | copy-start | bytes 2752516
  5.7 7.6 %copy-start.3 = (bf16[24,256]{1,0:T(8,128)(2,1)S(1)}, bf16[24,256]{1,0:T(8,128)(2,1)}, u32[]{:S(2)}) copy-start(bf16[24,256]{1,0:T(8,128)(2,1)} %maximum_bitcast_fusion.route_ref.refs_0_) | copy-start | bytes 36868
  5.7 33.3 %all-to-all-start.1 = ((bf16[8,2,40,1792]{3,2,1,0:T(8,128)(2,1)}), bf16[8,2,40,1792]{3,2,1,0:T(8,128)(2,1)}, u32[]{:S(2)}, u32[]{:S(2)}) async-start(bf16[8,2,40,1792]{3,2,1,0:T(8,128)(2,1)} %select.5), calls=%async_computation.1 | async-start | bytes 4587520 | tf_op jit(solution)/shard_map/all_to_all | solution.py:232
  11.0 24.0 %collective-permute-start.3 = (bf16[256,1792]{1,0:T(8,128)(2,1)S(1)}, bf16[256,1792]{1,0:T(8,128)(2,1)}, u32[]{:S(2)}, u32[]{:S(2)}) collective-permute-start(bf16[256,1792]{1,0:T(8,128)(2,1)S(1)} %bitcast.17), channel_id=1, source_target_pairs={{0,2},{1,3},{2,0},{3,1},{4,6},{5,7},{6,4},{7,5},{8,10},{9,11},{10,... | collective-permute-start | bytes 2752520 | tf_op jit(solution)/shard_map/ppermute | solution.py:229
  13.3 21.1 %collective-permute-start.2 = (bf16[24,256]{1,0:T(8,128)(2,1)S(1)}, bf16[24,256]{1,0:T(8,128)(2,1)S(1)}, u32[]{:S(2)}, u32[]{:S(2)}) collective-permute-start(bf16[24,256]{1,0:T(8,128)(2,1)S(1)} %copy-done.3), channel_id=1, source_target_pairs={{0,2},{1,3},{2,0},{3,1},{4,6},{5,7},{6,4},{7,5},{8,10},{9,11},{10,... | collective-permute-start | bytes 36872 | tf_op jit(solution)/shard_map/ppermute | solution.py:229
  34.4 0.6 copy-start.6
  38.6 4.7 %copy-start.1 = (bf16[1,1,256,1792]{3,2,1,0:T(8,128)(2,1)S(1)}, bf16[1,1,256,1792]{3,2,1,0:T(8,128)(2,1)}, u32[]{:S(2)}) copy-start(bf16[1,1,256,1792]{3,2,1,0:T(8,128)(2,1)} %param.10) | copy-start | bytes 2752516
  38.6 7.9 %copy-start.4 = (bf16[24,256]{1,0:T(8,128)(2,1)S(1)}, bf16[24,256]{1,0:T(8,128)(2,1)}, u32[]{:S(2)}) copy-start(bf16[24,256]{1,0:T(8,128)(2,1)} %maximum_bitcast_fusion.route_ref.refs_0_) | copy-start | bytes 36868
  38.9 52.8 %all-to-all-start.3 = ((bf16[8,2,40,1792]{3,2,1,0:T(8,128)(2,1)}), bf16[8,2,40,1792]{3,2,1,0:T(8,128)(2,1)}, u32[]{:S(2)}, u32[]{:S(2)}) async-start(bf16[8,2,40,1792]{3,2,1,0:T(8,128)(2,1)} %select.6), calls=%async_computation.3 | async-start | bytes 4587520 | tf_op jit(solution)/shard_map/all_to_all | solution.py:232
  43.3 44.8 %collective-permute-start.5 = (bf16[256,1792]{1,0:T(8,128)(2,1)S(1)}, bf16[256,1792]{1,0:T(8,128)(2,1)}, u32[]{:S(2)}, u32[]{:S(2)}) collective-permute-start(bf16[256,1792]{1,0:T(8,128)(2,1)S(1)} %bitcast.18), channel_id=1, source_target_pairs={{0,4},{1,5},{2,6},{3,7},{4,0},{5,1},{6,2},{7,3},{8,12},{9,13},{10,... | collective-permute-start | bytes 2752520 | tf_op jit(solution)/shard_map/ppermute | solution.py:229
  46.5 41.0 %collective-permute-start.4 = (bf16[24,256]{1,0:T(8,128)(2,1)S(1)}, bf16[24,256]{1,0:T(8,128)(2,1)S(1)}, u32[]{:S(2)}, u32[]{:S(2)}) collective-permute-start(bf16[24,256]{1,0:T(8,128)(2,1)S(1)} %copy-done.4), channel_id=1, source_target_pairs={{0,4},{1,5},{2,6},{3,7},{4,0},{5,1},{6,2},{7,3},{8,12},{9,13},{10,... | collective-permute-start | bytes 36872 | tf_op jit(solution)/shard_map/ppermute | solution.py:229
  87.5 0.6 copy-start.8
  91.8 4.5 %copy-start.2 = (bf16[1,1,256,1792]{3,2,1,0:T(8,128)(2,1)S(1)}, bf16[1,1,256,1792]{3,2,1,0:T(8,128)(2,1)}, u32[]{:S(2)}) copy-start(bf16[1,1,256,1792]{3,2,1,0:T(8,128)(2,1)} %param.10) | copy-start | bytes 2752516
  91.8 8.1 %copy-start.5 = (bf16[24,256]{1,0:T(8,128)(2,1)S(1)}, bf16[24,256]{1,0:T(8,128)(2,1)}, u32[]{:S(2)}) copy-start(bf16[24,256]{1,0:T(8,128)(2,1)} %maximum_bitcast_fusion.route_ref.refs_0_) | copy-start | bytes 36868
  91.8 33.5 %all-to-all-start.4 = ((bf16[8,2,40,1792]{3,2,1,0:T(8,128)(2,1)}), bf16[8,2,40,1792]{3,2,1,0:T(8,128)(2,1)}, u32[]{:S(2)}, u32[]{:S(2)}) async-start(bf16[8,2,40,1792]{3,2,1,0:T(8,128)(2,1)} %select.7), calls=%async_computation.4 | async-start | bytes 4587520 | tf_op jit(solution)/shard_map/all_to_all | solution.py:232
  96.3 25.4 %collective-permute-start.1 = (bf16[256,1792]{1,0:T(8,128)(2,1)S(1)}, bf16[256,1792]{1,0:T(8,128)(2,1)}, u32[]{:S(2)}, u32[]{:S(2)}) collective-permute-start(bf16[256,1792]{1,0:T(8,128)(2,1)S(1)} %bitcast.19), channel_id=1, source_target_pairs={{0,6},{1,7},{2,4},{3,5},{4,2},{5,3},{6,0},{7,1},{8,14},{9,15},{10,... | collective-permute-start | bytes 2752520 | tf_op jit(solution)/shard_map/ppermute | solution.py:229
  99.9 21.2 %collective-permute-start = (bf16[24,256]{1,0:T(8,128)(2,1)S(1)}, bf16[24,256]{1,0:T(8,128)(2,1)S(1)}, u32[]{:S(2)}, u32[]{:S(2)}) collective-permute-start(bf16[24,256]{1,0:T(8,128)(2,1)S(1)} %copy-done.5), channel_id=1, source_target_pairs={{0,6},{1,7},{2,4},{3,5},{4,2},{5,3},{6,0},{7,1},{8,14},{9,15},{10,... | collective-permute-start | bytes 36872 | tf_op jit(solution)/shard_map/ppermute | solution.py:229
  121.1 0.6 copy-start.7
  125.3 48.4 %all-to-all-start = ((bf16[8,2,40,1792]{3,2,1,0:T(8,128)(2,1)}), bf16[8,2,40,1792]{3,2,1,0:T(8,128)(2,1)}, u32[]{:S(2)}, u32[]{:S(2)}) async-start(bf16[8,2,40,1792]{3,2,1,0:T(8,128)(2,1)} %select.4), calls=%async_computation | async-start | bytes 4587520 | tf_op jit(solution)/shard_map/all_to_all | solution.py:232
  173.7 57.0 %all-to-all-start.5 = ((bf16[8,2,80,1792]{3,2,1,0:T(8,128)(2,1)}), bf16[8,2,80,1792]{3,2,1,0:T(8,128)(2,1)}, u32[]{:S(2)}, u32[]{:S(2)}) async-start(bf16[8,2,80,1792]{3,2,1,0:T(8,128)(2,1)} %experts.3), calls=%async_computation.5 | async-start | bytes 9175040 | tf_op jit(solution)/shard_map/all_to_all | solution.py:232
  230.8 77.0 %all-to-all-start.6 = ((bf16[8,2,40,1792]{3,2,1,0:T(8,128)(2,1)}), bf16[8,2,40,1792]{3,2,1,0:T(8,128)(2,1)}, u32[]{:S(2)}, u32[]{:S(2)}) async-start(bf16[8,2,40,1792]{3,2,1,0:T(8,128)(2,1)} %get-tuple-element.11), calls=%async_computation.6 | async-start | bytes 4587520 | tf_op jit(solution)/shard_map/all_to_all | solution.py:232
  289.0 64.2 %collective-permute-start.7 = (bf16[256,1792]{1,0:T(8,128)(2,1)}, bf16[256,1792]{1,0:T(8,128)(2,1)}, u32[]{:S(2)}, u32[]{:S(2)}) collective-permute-start(bf16[256,1792]{1,0:T(8,128)(2,1)} %get-tuple-element.12), channel_id=1, source_target_pairs={{0,2},{1,3},{2,0},{3,1},{4,6},{5,7},{6,4},{7,5},{8,10},{9,11},{10,... | collective-permute-start | bytes 2752520 | tf_op jit(solution)/shard_map/ppermute | solution.py:229
  307.8 72.5 %all-to-all-start.2 = ((bf16[8,2,40,1792]{3,2,1,0:T(8,128)(2,1)}), bf16[8,2,40,1792]{3,2,1,0:T(8,128)(2,1)}, u32[]{:S(2)}, u32[]{:S(2)}) async-start(bf16[8,2,40,1792]{3,2,1,0:T(8,128)(2,1)} %get-tuple-element.9), calls=%async_computation.2 | async-start | bytes 4587520 | tf_op jit(solution)/shard_map/all_to_all | solution.py:232
  353.2 42.4 %collective-permute-start.6 = (bf16[256,1792]{1,0:T(8,128)(2,1)}, bf16[256,1792]{1,0:T(8,128)(2,1)}, u32[]{:S(2)}, u32[]{:S(2)}) collective-permute-start(bf16[256,1792]{1,0:T(8,128)(2,1)} %get-tuple-element.10), channel_id=1, source_target_pairs={{0,2},{1,3},{2,0},{3,1},{4,6},{5,7},{6,4},{7,5},{8,10},{9,11},{10,... | collective-permute-start | bytes 2752520 | tf_op jit(solution)/shard_map/ppermute | solution.py:229
  357.0 38.6 %collective-permute-start.8 = (bf16[256,1792]{1,0:T(8,128)(2,1)}, bf16[256,1792]{1,0:T(8,128)(2,1)}, u32[]{:S(2)}, u32[]{:S(2)}) collective-permute-start(bf16[256,1792]{1,0:T(8,128)(2,1)} %combine.4), channel_id=1, source_target_pairs={{0,6},{1,7},{2,4},{3,5},{4,2},{5,3},{6,0},{7,1},{8,14},{9,15},{10,... | collective-permute-start | bytes 2752520 | tf_op jit(solution)/shard_map/ppermute | solution.py:229
